TPU v7x, 128 devices: a whole 4x4x4 slice. The times are simulated.
128 devices in a mesh: rows: 64 (over y_lo, x, z, core), chan: 2 (over y_hi).
Axes of the slice: x: 4, y: 4 (y_hi: 2, y_lo: 2; y = y_hi * 2 + y_lo), z: 4, core: 2. Of those that a mesh axis runs over, the one named last changes fastest.
Arguments:
- pixels: float32 [4096, 16384], P(('chan', 'rows')), parts along dimension 0, may hold values from -6 to 6
- row_taps: float32 [32768], P(('chan', 'rows')), parts along dimension 0, may hold values from -0.046875 to 0.046875
- column_taps: float32 [4096], P(('chan', 'rows')), parts along dimension 0, may hold values from -0.125 to 0.125
- stencil: float32 [6, 3], P('chan'), parts along dimension 0, may hold values from -3 to 3
Outputs:
- filtered: float32 [4096, 16384], P(('chan', 'rows')), parts along dimension 0
There are 2 independent parts, one for each index of `chan`. A program takes and returns all parts, laid end to end along the dimension named above; each array names one. Nothing has to cross between parts.
All inputs are finite; a program needn't handle non-finite values.
Results may differ from a plain program's by a relative error of at most 0.0003.
Values sent between devices are 32-bit elements; how exact they have to be, the bound alone decides.
A program may use at most 128 MiB of HBM per device.

v0:
```python
import math

import jax
import jax.numpy as jnp
from jax import lax
from jax.sharding import PartitionSpec as P

dft_precision = lax.Precision.HIGH
row_forms = ("kj,rjm->rkm", "rkm,ml->rkl")
column_forms = ("kj,jmc->kmc", "kmc,ml->klc")


def joined_along(pieces, dim):
    shape = list(pieces.shape[1:])
    shape[dim] *= pieces.shape[0]
    return jnp.moveaxis(pieces, 0, dim).reshape(shape)


def from_everyone(shard, axis):
    count = lax.axis_size(axis)
    return lax.all_to_all(
        jnp.broadcast_to(shard[None], (count, *shard.shape)), axis, 0, 0, tiled=True
    )


def collect(shard, axis, dim):
    return joined_along(from_everyone(shard, axis), dim)


def padded_2(cells, sides, width):
    for axis, dim in sides:
        count = lax.axis_size(axis)
        head = lax.slice_in_dim(cells, 0, width, axis=dim)
        tail = lax.slice_in_dim(cells, cells.shape[dim] - width, cells.shape[dim], axis=dim)
        cells = jnp.concatenate(
            [
                lax.ppermute(tail, axis, [(i, (i + 1) % count) for i in range(count)]),
                cells,
                lax.ppermute(head, axis, [((i + 1) % count, i) for i in range(count)]),
            ],
            axis=dim,
        )
    return cells


def split_length(length):
    factor = int(math.isqrt(length))
    while length % factor:
        factor -= 1
    return (length // factor, factor)


def dft_tables(length):
    positions = jnp.arange(length, dtype=jnp.int32)
    product = positions[:, None] * positions[None, :] % length
    angles = product.astype(jnp.float32) * (2.0 * math.pi / length)
    return (jnp.cos(angles), -jnp.sin(angles))


def prepare(length, twist_shape):
    outer_len, inner_len = split_length(length)
    cos_outer, sin_outer = dft_tables(outer_len)
    cos_inner, sin_inner = dft_tables(inner_len)
    outer_pos = jnp.arange(outer_len, dtype=jnp.int32)
    inner_pos = jnp.arange(inner_len, dtype=jnp.int32)
    product = outer_pos[:, None] * inner_pos[None, :] % length
    angles = product.astype(jnp.float32) * (2.0 * math.pi / length)
    twist_real = jnp.cos(angles).reshape(twist_shape)
    twist_imag = (-jnp.sin(angles)).reshape(twist_shape)
    return (
        outer_len,
        inner_len,
        cos_outer,
        sin_outer,
        cos_inner,
        sin_inner,
        twist_real,
        twist_imag,
    )


def contract(form, left, right):
    return jnp.einsum(
        form, left, right, precision=dft_precision, preferred_element_type=jnp.float32
    )


def forward(values, tables, forms):
    outer_len, inner_len, cos_outer, sin_outer, cos_inner, sin_inner, twist_real, twist_imag = (
        tables
    )
    first_real = contract(forms[0], cos_outer, values)
    first_imag = contract(forms[0], sin_outer, values)
    turned_real = first_real * twist_real - first_imag * twist_imag
    turned_imag = first_real * twist_imag + first_imag * twist_real
    out_real = contract(forms[1], turned_real, cos_inner) - contract(
        forms[1], turned_imag, sin_inner
    )
    out_imag = contract(forms[1], turned_real, sin_inner) + contract(
        forms[1], turned_imag, cos_inner
    )
    return (out_real, out_imag)


def inverse(spec_real, spec_imag, tables, forms):
    outer_len, inner_len, cos_outer, sin_outer, cos_inner, sin_inner, twist_real, twist_imag = (
        tables
    )
    back_real = contract(forms[1], spec_real, cos_inner) + contract(forms[1], spec_imag, sin_inner)
    back_imag = contract(forms[1], spec_imag, cos_inner) - contract(forms[1], spec_real, sin_inner)
    turned_real = back_real * twist_real + back_imag * twist_imag
    turned_imag = back_imag * twist_real - back_real * twist_imag
    result = contract(forms[0], cos_outer, turned_real) + contract(forms[0], sin_outer, turned_imag)
    return result / float(outer_len * inner_len)


def convolve(values, filter_spec, tables, forms):
    spec_real, spec_imag = forward(values, tables, forms)
    filter_real, filter_imag = filter_spec
    prod_real = spec_real * filter_real - spec_imag * filter_imag
    prod_imag = spec_real * filter_imag + spec_imag * filter_real
    return inverse(prod_real, prod_imag, tables, forms)


def body(pixels, row_taps, column_taps, stencil):
    rows_dev, row_length = pixels.shape
    devices_rows = lax.axis_size("rows")
    whole_row, whole_column = (collect(row_taps, "rows", 0), collect(column_taps, "rows", 0))
    column_length = whole_column.shape[0]
    row_tables = prepare(row_length, (1, split_length(row_length)[0], split_length(row_length)[1]))
    column_tables = prepare(
        column_length, (split_length(column_length)[0], split_length(column_length)[1], 1)
    )
    row_filter = forward(whole_row.reshape(1, row_tables[0], row_tables[1]), row_tables, row_forms)
    column_filter = forward(
        whole_column.reshape(column_tables[0], column_tables[1], 1), column_tables, column_forms
    )
    cols_dev = row_length // devices_rows
    lane_width = min(128, cols_dev)
    groups = cols_dev // lane_width
    padded = padded_2(pixels, (("rows", 0),), 1)
    shaped = pixels.reshape(pixels.shape[0], row_tables[0], row_tables[1])
    blocks = (
        convolve(shaped, row_filter, row_tables, row_forms)
        .reshape(pixels.shape)
        .reshape(rows_dev, groups, devices_rows * lane_width)
    )
    moved = lax.all_to_all(blocks, "rows", split_axis=2, concat_axis=0, tiled=True)
    shaped = moved.reshape(column_tables[0], column_tables[1], -1)
    result = lax.all_to_all(
        convolve(shaped, column_filter, column_tables, column_forms).reshape(moved.shape),
        "rows",
        split_axis=0,
        concat_axis=2,
        tiled=True,
    )
    convolved = result.reshape(rows_dev, row_length)
    filtered = convolved
    for offset_row in range(3):
        row_band = padded[offset_row : offset_row + rows_dev]
        for offset_col in range(3):
            filtered = filtered + stencil[offset_row, offset_col] * jnp.roll(
                row_band, 1 - offset_col, axis=1
            )
    return filtered


def solution(mesh):
    in_specs = (
        P(("chan", "rows"), None),
        P(("chan", "rows")),
        P(("chan", "rows")),
        P("chan", None),
    )
    out_specs = P(("chan", "rows"), None)
    return jax.shard_map(body, mesh=mesh, in_specs=in_specs, out_specs=out_specs, check_vma=False)
```

profile of v0, /device:TPU:1, one launch (start us, length us, event | category | flops | bytes accessed | tf_op | source)
XLA Modules:
  0.0 261.1 jit_solution(14520849372788096148)
XLA Ops:
  0.0 1.3 broadcast_in_dim.5
  1.3 10.8 %all-to-all-start.2 = ((f32[64,1,32]{2,1,0:T(1,128)}), f32[64,1,32]{2,1,0:T(1,128)S(1)}, u32[]{:S(2)}, u32[]{:S(2)}) async-start(f32[64,1,32]{2,1,0:T(1,128)} %broadcast_in_dim.5), calls=%async_computation.2 | async-start | bytes 65536 | tf_op jit(solution)/shard_map/all_to_all | solution.py:21
  12.1 1.3 fusion.356
  13.4 1.7 collective-permute-start
  15.4 2.0 copy.88
  17.4 1.2 fusion.102
  18.6 1.2 fusion.109
  19.9 1.4 fusion.26
  21.3 1.4 fusion.24
  22.8 1.5 constant_dynamic-update-slice_fusion
  24.5 2.7 %fusion.56 = f32[32,128,128]{2,1,0:T(8,128)} fusion(f32[32,128,128]{2,1,0:T(8,128)S(1)} %fusion.26, f32[128,32,128]{2,0,1:T(8,128)S(1)} %fusion.102, f32[128,32,128]{2,0,1:T(8,128)S(1)} %fusion.109, f32[128,128]{1,0:T(8,128)S(1)} %get-tuple-element.30, f32[128,128]{1,0:T(8,128)S(1)} %get-tuple-element.31), kind=kOutput, calls=%fused_computation.80 | convolution fusion | flops 404979712 | bytes 8519680 | tf_op jit(solution)/shard_map/rkm,ml->rkl/dot_general | solution.py:83
  27.2 2.7 %fusion.59 = f32[32,128,128]{2,1,0:T(8,128)} fusion(f32[32,128,128]{2,1,0:T(8,128)S(1)} %fusion.24, f32[128,32,128]{2,0,1:T(8,128)S(1)} %fusion.102, f32[128,32,128]{2,0,1:T(8,128)S(1)} %fusion.109, f32[128,128]{1,0:T(8,128)S(1)} %get-tuple-element.30, f32[128,128]{1,0:T(8,128)S(1)} %get-tuple-element.31), kind=kOutput, calls=%fused_computation.81 | convolution fusion | flops 404996096 | bytes 8519680 | tf_op jit(solution)/shard_map/rkm,ml->rkl/dot_general | solution.py:83
  29.9 0.7 fusion.357
  30.6 0.7 broadcast_in_dim.4
  31.2 9.3 %all-to-all-start = ((f32[64,1,256]{2,1,0:T(1,128)}), f32[64,1,256]{2,1,0:T(1,128)S(1)}, u32[]{:S(2)}, u32[]{:S(2)}) async-start(f32[64,1,256]{2,1,0:T(1,128)} %broadcast_in_dim.4), calls=%async_computation | async-start | bytes 131072 | tf_op jit(solution)/shard_map/all_to_all | solution.py:21
  40.8 0.3 fusion.169
  42.3 6.1 %all-to-all-done = f32[64,1,256]{2,1,0:T(1,128)S(1)} async-done(((f32[64,1,256]{2,1,0:T(1,128)}), f32[64,1,256]{2,1,0:T(1,128)S(1)}, u32[]{:S(2)}, u32[]{:S(2)}) %all-to-all-start) | async-done | bytes 65568 | tf_op jit(solution)/shard_map/all_to_all | solution.py:21
  48.4 0.4 convolution_bitcast_fusion
  48.9 0.4 convolution_bitcast_fusion.1
  49.3 0.7 fusion.93
  49.9 0.7 fusion.95
  50.6 0.7 convolution_add_fusion.1
  51.3 0.7 convolution_subtract_fusion.1
  52.0 3.1 %fusion.83 = f32[32,128,128]{2,1,0:T(8,128)S(1)} fusion(f32[32,128,128]{2,1,0:T(8,128)} %fusion.59, f32[32,128,128]{2,1,0:T(8,128)S(1)} %copy-done.1, f32[128,128]{1,0:T(8,128)S(1)} %convolution_add_fusion.1, f32[128,128]{1,0:T(8,128)S(1)} %convolution_subtract_fusion.1), kind=kOutput, calls=%fused_computation.105 | convolution fusion | flops 404455424 | bytes 6422528 | tf_op jit(solution)/shard_map/rkm,ml->rkl/dot_general | solution.py:83
  55.1 1.3 fusion.82
  56.4 1.4 convolution_subtract_fusion
  57.8 1.4 convolution_add_fusion
  59.2 2.1 fusion.32
  61.2 14.2 %multiply_bitcast_fusion = f32[32,128,128]{1,2,0:T(8,128)} fusion(f32[32,128,128]{2,1,0:T(8,128)S(1)} %fusion.32, f32[32,128,128]{2,1,0:T(8,128)S(1)} %convolution_subtract_fusion, f32[32,128,128]{2,1,0:T(8,128)S(1)} %convolution_add_fusion, f32[128,128]{1,0:T(8,128)S(1)} %get-tuple-element.30, f32[128,128]{1,0:T(8,128)S(1)} %get-tuple-element.31), kind=kOutput, calls=%fused_computation.57 | convolution fusion | flops 405504000 | bytes 8519680 | tf_op jit(solution)/shard_map/kj,rjm->rkm/dot_general | solution.py:83
  75.4 2.9 %copy.70 = f32[32,128,128]{2,1,0:T(8,128)} copy(f32[32,128,128]{1,2,0:T(8,128)} %multiply_bitcast_fusion) | data formatting | bytes 4194304 | tf_op jit(solution)/shard_map/div | solution.py:114
  78.3 3.4 %reshape_reshape.2 = f32[32,2,8192]{2,1,0:T(2,128)} reshape(f32[32,128,128]{2,1,0:T(8,128)} %copy.70) | data formatting | bytes 4194304 | tf_op jit(solution)/shard_map/reshape;reshape | solution.py:146
  81.7 11.8 %copy.71 = f32[32,2,8192]{0,1,2:T(2,128)} copy(f32[32,2,8192]{2,1,0:T(2,128)} %reshape_reshape.2) | data formatting | bytes 4194304 | tf_op jit(solution)/shard_map/reshape;reshape | solution.py:146
  93.6 10.8 %reshape.206 = f32[64,1,8192]{2,1,0:T(1,128)} reshape(f32[8192,2,32]{2,1,0:T(2,128)} %bitcast.187) | data formatting | bytes 4194304
  104.4 5.3 %all-to-all-start.1 = ((f32[64,1,8192]{2,1,0:T(1,128)}), f32[64,1,8192]{2,1,0:T(1,128)}, u32[]{:S(2)}, u32[]{:S(2)}) async-start(f32[64,1,8192]{2,1,0:T(1,128)} %reshape.206), calls=%async_computation.1 | async-start | bytes 4194304 | tf_op jit(solution)/shard_map/all_to_all | solution.py:148
  109.7 1.9 dynamic-update-slice.1
  111.7 0.8 fusion.353
  112.5 4.8 %fusion.354 = (f32[32,16383]{1,0:T(8,128)}, f32[32,16383]{1,0:T(8,128)}, f32[32,16383]{1,0:T(8,128)}, f32[32,16383]{1,0:T(8,128)}) fusion(f32[32,16384]{1,0:T(8,128)S(1)} %copy-done, f32[1,16384]{1,0:T(1,128)S(1)} %collective-permute-done), kind=kLoop, calls=%fused_computation.384 | loop fusion | flops 1048512 | bytes 14745088 | tf_op jit(solution)/shard_map/jit(_roll_static)/slice | solution.py:162
  117.3 20.7 %all-to-all-done.1 = f32[64,1,8192]{2,1,0:T(1,128)} async-done(((f32[64,1,8192]{2,1,0:T(1,128)}), f32[64,1,8192]{2,1,0:T(1,128)}, u32[]{:S(2)}, u32[]{:S(2)}) %all-to-all-start.1) | async-done | bytes 2097184 | tf_op jit(solution)/shard_map/all_to_all | solution.py:148
  138.0 0.5 broadcast.386
  138.6 8.8 %reduce = f32[64,8192]{1,0:T(8,128)} reduce(f32[64,1,8192]{2,1,0:T(1,128)} %all-to-all-done.1, f32[]{:T(128)} %broadcast.386), dimensions={1}, to_apply=%all_to_all.33.reduce_sub_computation | reduce | bytes 4194308 | tf_op jit(solution)/shard_map/all_to_all | solution.py:148
  147.4 9.5 %reshape.207 = f32[8192,2,32]{2,1,0:T(2,128)} reshape(f32[64,8192]{1,0:T(8,128)} %reduce) | data formatting | bytes 4194304
  156.9 11.6 %copy.72 = f32[32,2,64,128]{3,1,2,0:T(2,128)} copy(f32[32,2,64,128]{0,1,3,2:T(2,128)} %bitcast.188) | data formatting | bytes 4194304 | tf_op jit(solution)/shard_map/all_to_all | solution.py:148
  168.6 4.3 %reshape.197 = f32[64,32,256]{2,0,1:T(8,128)} reshape(f32[64,32,2,128]{3,2,0,1:T(2,128)} %bitcast.192) | data formatting | bytes 4194304 | tf_op jit(solution)/shard_map/reshape | solution.py:149
  172.9 2.8 %fusion.128 = f32[64,32,256]{2,0,1:T(8,128)S(1)} fusion(f32[64,32,256]{2,0,1:T(8,128)} %reshape.197), kind=kOutput, calls=%fused_computation.167 | convolution fusion | flops 201383936 | bytes 4194304 | tf_op jit(solution)/shard_map/kj,jmc->kmc/dot_general | solution.py:83
  175.7 1.9 multiply_subtract_fusion
  177.6 2.2 fusion.42
  179.8 2.2 fusion.40
  182.0 2.2 fusion.48
  184.2 2.2 fusion.51
  186.4 1.5 fusion.74
  187.9 1.3 fusion.78
  189.2 1.3 fusion.80
  190.5 1.3 fusion.76
  191.8 5.8 %fusion.17 = f32[64,32,256]{2,0,1:T(8,128)S(1)} fusion(f32[64,32]{0,1:T(8,128)S(1)} %get-tuple-element.32, f32[64,32]{0,1:T(8,128)S(1)} %get-tuple-element.33, f32[32,64,256]{2,0,1:T(8,128)S(1)} %fusion.76, f32[32,64,256]{2,0,1:T(8,128)S(1)} %fusion.80, f32[32,64,256]{2,0,1:T(8,128)S(1)} %fusion.78, f32[32,64,256]{2,0,1:T(8,128)S(1)} %fusion.74), kind=kOutput, calls=%fused_computation.33 | convolution fusion | flops 204005376 | bytes 10502144 | tf_op jit(solution)/shard_map/kj,jmc->kmc/dot_general | solution.py:83
  197.6 6.0 %add_multiply_fusion = f32[64,32,256]{2,0,1:T(8,128)S(1)} fusion(f32[64,32,256]{2,0,1:T(8,128)S(1)} %fusion.17, f32[64,32]{0,1:T(8,128)S(1)} %get-tuple-element.32, f32[64,32]{0,1:T(8,128)S(1)} %get-tuple-element.33, f32[32,64,256]{2,0,1:T(8,128)S(1)} %fusion.76, f32[32,64,256]{2,0,1:T(8,128)S(1)} %fusion.80, f32[32,64,256]{2,0,1:T(8,128)S(1)} %fusion.78, ...), kind=kOutput, calls=%fused_computation.54 | convolution fusion | flops 205058048 | bytes 12599296 | tf_op jit(solution)/shard_map/kj,jmc->kmc/dot_general | solution.py:83
  203.6 2.5 copy.83
  206.1 3.3 %reshape.198 = f32[2048,2,128]{2,1,0:T(2,128)} reshape(f32[64,32,256]{2,1,0:T(8,128)} %copy.83) | data formatting | bytes 4194304 | tf_op jit(solution)/shard_map/reshape | solution.py:151
  209.5 5.9 %all-to-all-start.3 = ((f32[2048,2,128]{2,1,0:T(2,128)}), f32[2048,2,128]{2,1,0:T(2,128)}, u32[]{:S(2)}, u32[]{:S(2)}) async-start(f32[2048,2,128]{2,1,0:T(2,128)} %reshape.198), calls=%async_computation.3 | async-start | bytes 4194304 | tf_op jit(solution)/shard_map/all_to_all | solution.py:150
  215.4 5.2 %fusion.352 = (f32[32,16383]{1,0:T(8,128)}, f32[32,16383]{1,0:T(8,128)}) fusion(f32[33,16384]{1,0:T(8,128)} %dynamic-update-slice.1), kind=kLoop, calls=%fused_computation.382 | loop fusion | bytes 8388096 | tf_op jit(solution)/shard_map/jit(_roll_static)/slice | solution.py:162
  220.6 23.1 %all-to-all-done.3 = f32[2048,2,128]{2,1,0:T(2,128)} async-done(((f32[2048,2,128]{2,1,0:T(2,128)}), f32[2048,2,128]{2,1,0:T(2,128)}, u32[]{:S(2)}, u32[]{:S(2)}) %all-to-all-start.3) | async-done | bytes 2097184 | tf_op jit(solution)/shard_map/all_to_all | solution.py:150
  243.7 1.9 copy.84
  245.5 1.2 copy.85
  246.8 0.7 copy-done.3
  247.5 13.3 %fusion.11 = f32[32,16384]{1,0:T(8,128)} fusion(f32[32,16384]{1,0:T(8,128)S(1)} %copy-done, f32[1,16384]{1,0:T(1,128)S(1)} %collective-permute-done, f32[4,8,128,128]{3,2,1,0:T(8,128)S(1)} %bitcast.191, f32[33,16384]{1,0:T(8,128)S(1)} %copy-done.3, f32[32,16383]{1,0:T(8,128)} %get-tuple-element.15, f32[32,16383]{1,0:T(8,128)} %get-tuple-element.16, ...), kind=kLoop, calls=%fused_computation.17 | loop fusion | flops 14155776 | bytes 21036836 | tf_op jit(solution)/shard_map/add | solution.py:162
  (31 shorter events, 2.2 us)
Async XLA Ops:
  1.3 29.3 %all-to-all-start.2 = ((f32[64,1,32]{2,1,0:T(1,128)}), f32[64,1,32]{2,1,0:T(1,128)S(1)}, u32[]{:S(2)}, u32[]{:S(2)}) async-start(f32[64,1,32]{2,1,0:T(1,128)} %broadcast_in_dim.5), calls=%async_computation.2 | async-start | bytes 65536 | tf_op jit(solution)/shard_map/all_to_all | solution.py:21
  13.4 99.1 %collective-permute-start = (f32[1,16384]{1,0:T(1,128)S(1)}, f32[1,16384]{1,0:T(1,128)S(1)}, u32[]{:S(2)}, u32[]{:S(2)}) collective-permute-start(f32[1,16384]{1,0:T(1,128)S(1)} %get-tuple-element.20), channel_id=1, source_target_pairs={{0,2},{2,4},{4,6},{6,8},{8,10},{10,12},{12,14},{14,16},{16,18},{18... | collective-permute-start | bytes 196616 | tf_op jit(solution)/shard_map/ppermute | solution.py:37
  15.1 94.6 %collective-permute-start.1 = (f32[1,16384]{1,0:T(1,128)S(1)}, f32[1,16384]{1,0:T(1,128)S(1)}, u32[]{:S(2)}, u32[]{:S(2)}) collective-permute-start(f32[1,16384]{1,0:T(1,128)S(1)} %get-tuple-element.19), channel_id=1, source_target_pairs={{2,0},{4,2},{6,4},{8,6},{10,8},{12,10},{14,12},{16,14},{18,16},{20... | collective-permute-start | bytes 196616 | tf_op jit(solution)/shard_map/ppermute | solution.py:39
  21.3 1.6 copy-start
  27.2 2.7 %copy-start.7 = (f32[3,3]{1,0:T(4,128)S(1)}, f32[3,3]{1,0:T(4,128)}, u32[]{:S(2)}) copy-start(f32[3,3]{1,0:T(4,128)} %param.7) | copy-start | bytes 112
  27.2 3.4 %copy-start.8 = (f32[256]{0:T(256)S(1)}, f32[256]{0:T(256)}, u32[]{:S(2)}) copy-start(f32[256]{0:T(256)} %param.5) | copy-start | bytes 3076
  31.2 17.2 %all-to-all-start = ((f32[64,1,256]{2,1,0:T(1,128)}), f32[64,1,256]{2,1,0:T(1,128)S(1)}, u32[]{:S(2)}, u32[]{:S(2)}) async-start(f32[64,1,256]{2,1,0:T(1,128)} %broadcast_in_dim.4), calls=%async_computation | async-start | bytes 131072 | tf_op jit(solution)/shard_map/all_to_all | solution.py:21
  48.4 3.5 %copy-start.1 = (f32[32,128,128]{2,1,0:T(8,128)S(1)}, f32[32,128,128]{2,1,0:T(8,128)}, u32[]{:S(2)}) copy-start(f32[32,128,128]{2,1,0:T(8,128)} %fusion.56) | copy-start | bytes 6291460
  52.0 3.1 %copy-start.2 = (f32[32,128,128]{2,1,0:T(8,128)S(1)}, f32[32,128,128]{2,1,0:T(8,128)}, u32[]{:S(2)}) copy-start(f32[32,128,128]{2,1,0:T(8,128)} %fusion.59) | copy-start | bytes 6291460
  104.4 33.6 %all-to-all-start.1 = ((f32[64,1,8192]{2,1,0:T(1,128)}), f32[64,1,8192]{2,1,0:T(1,128)}, u32[]{:S(2)}, u32[]{:S(2)}) async-start(f32[64,1,8192]{2,1,0:T(1,128)} %reshape.206), calls=%async_computation.1 | async-start | bytes 4194304 | tf_op jit(solution)/shard_map/all_to_all | solution.py:148
  172.8 2.9 %copy-start.4 = (f32[64,32,256]{2,0,1:T(8,128)S(1)}, f32[64,32,256]{2,0,1:T(8,128)}, u32[]{:S(2)}) copy-start(f32[64,32,256]{2,0,1:T(8,128)} %reshape.197) | copy-start | bytes 6291460
  209.5 34.2 %all-to-all-start.3 = ((f32[2048,2,128]{2,1,0:T(2,128)}), f32[2048,2,128]{2,1,0:T(2,128)}, u32[]{:S(2)}, u32[]{:S(2)}) async-start(f32[2048,2,128]{2,1,0:T(2,128)} %reshape.198), calls=%async_computation.3 | async-start | bytes 4194304 | tf_op jit(solution)/shard_map/all_to_all | solution.py:150
  243.6 3.1 %copy-start.5 = (f32[32,16383]{1,0:T(8,128)S(1)}, f32[32,16383]{1,0:T(8,128)}, u32[]{:S(2)}) copy-start(f32[32,16383]{1,0:T(8,128)} %get-tuple-element.13) | copy-start | bytes 6291076
  243.7 3.1 %copy-start.6 = (f32[32,16383]{1,0:T(8,128)S(1)}, f32[32,16383]{1,0:T(8,128)}, u32[]{:S(2)}) copy-start(f32[32,16383]{1,0:T(8,128)} %get-tuple-element.14) | copy-start | bytes 6291076
  245.5 2.0 copy-start.3
where the time goes:
time: 266 us; the launch traced here: 261 us
  local copies, waits for them, and re-layouts  80.5 us (30%)
  matrix products  69.8 us (26%)
  waiting for transfers between devices  49.9 us (19%)
  starting transfers between devices  33 us (12%)
  other arithmetic  27.4 us (10%)
    dot_general x36, matrix products, contract(): jnp.einsum(form, left, right, precision=dft_precision, preferred_element_...  69.8 us
    unnamed x22, local copies, waits for them, and re-layouts  24.8 us
    all_to_all x1, waiting for transfers between devices, body(): lax.all_to_all(convolve(shaped, column_filter, column_tables, column_form...  23.1 us
    all_to_all x1, waiting for transfers between devices, body(): lax.all_to_all(blocks, 'rows', split_axis=2, concat_axis=0, tiled=True)  20.7 us
    all_to_all x2, starting transfers between devices, from_everyone(): lax.all_to_all(jnp.broadcast_to(shard[None], (count, *shard.shape)), axis...  20.1 us
    another operation x2, local copies, waits for them, and re-layouts, body(): blocks = convolve(shaped, row_filter, row_tables, row_forms).reshape(pixe...  15.2 us
    add x1, other arithmetic, body(): filtered + stencil[offset_row, offset_col] * jnp.roll(row_band, 1 - offse...  13.3 us
    all_to_all x2, local copies, waits for them, and re-layouts, body(): lax.all_to_all(blocks, 'rows', split_axis=2, concat_axis=0, tiled=True)  12.2 us
  transfers between devices with their start and end apart: 6, of which 3 were waited for; matrix products, arithmetic and copies ran while one was open for 34% of the time, Pallas kernels for 0%

commit v1 on v0

v1 whole, which is shorter than its diff:
```python
import functools
import math

import jax
import jax.numpy as jnp
import ml_dtypes
import numpy as np
from jax import lax
from jax.experimental import pallas as pl
from jax.experimental.pallas import tpu as pltpu
from jax.sharding import PartitionSpec as P

MESH = pl.DeviceIdType.MESH
F32, BF16 = jnp.float32, jnp.bfloat16
PEERS = 64
LANES = 128
BLOCKS = 16
GROUP = 7


def split_np(values):
    high = values.astype(ml_dtypes.bfloat16)
    low = (values - high.astype(np.float64)).astype(ml_dtypes.bfloat16)
    return high, low


def plane_tables():
    pos = np.arange(LANES)
    fwd = np.zeros((LANES, LANES))
    inv = np.zeros((LANES, LANES))
    for s in range(PEERS):
        angle = 2 * np.pi * (pos * s % LANES) / LANES
        if s == 0:
            fwd[0], fwd[1] = 1.0, (-1.0) ** pos
            inv[:, 0], inv[:, 1] = 1.0 / LANES, (-1.0) ** pos / LANES
        else:
            fwd[2 * s], fwd[2 * s + 1] = np.cos(angle), -np.sin(angle)
            inv[:, 2 * s], inv[:, 2 * s + 1] = 2 * np.cos(angle) / LANES, -2 * np.sin(angle) / LANES
    stacked = []
    for table in (fwd, inv):
        high, low = split_np(table)
        stacked.append(np.block([[high, high], [low, low]]))
    return stacked


def tap_tables():
    tab = np.zeros((PEERS, 8, 2 * LANES), np.float64)
    pos = np.arange(LANES)
    cols = 4 * (pos // 2) + pos % 2
    for s in range(PEERS):
        for row, freq in ((0, s), (2, s if s else LANES // 2)):
            angle = 2 * np.pi * (pos * freq % LANES) / LANES
            tab[s, row, cols], tab[s, row + 1, cols] = np.cos(angle), -np.sin(angle)
            turn = 2 * np.pi * freq / LANES
            tab[s, 4 + row], tab[s, 5 + row] = np.cos(turn), -np.sin(turn)
    return tab.astype(np.float32)


def turned(k, n, re, im, sign):
    angle = 2 * math.pi * k / n
    c, s = math.cos(angle), sign * math.sin(angle)
    if k == 0:
        return re, im
    if 4 * k == n:
        return (-im, re) if sign > 0 else (im, -re)
    if 8 * k == n:
        return (re - s / abs(s) * im) * c, (im + s / abs(s) * re) * c
    return re * c - im * s, re * s + im * c


def rfft(values):
    n = len(values)
    if n == 2:
        return [(values[0] + values[1], None), (values[0] - values[1], None)]
    even, odd = rfft(values[0::2]), rfft(values[1::2])
    out = [None] * (n // 2 + 1)
    for k in range(n // 4 + 1):
        er, ei = even[k]
        orr, oi = odd[k]
        if k == 0:
            out[0], out[n // 2] = (er + orr, None), (er - orr, None)
        elif 4 * k == n:
            out[k] = (er, -orr)
        else:
            tr, ti = turned(k, n, orr, oi, -1)
            out[k] = (er + tr, ei + ti)
            out[n // 2 - k] = (er - tr, ti - ei)
    return out


def irfft(spectrum):
    n = 2 * (len(spectrum) - 1)
    if n == 2:
        a, b = spectrum[0][0], spectrum[1][0]
        return [a + b, a - b]
    even, odd = [None] * (n // 4 + 1), [None] * (n // 4 + 1)
    for k in range(n // 4 + 1):
        ar, ai = spectrum[k]
        br, bi = spectrum[n // 2 - k]
        if k == 0:
            even[0], odd[0] = (ar + br, None), (ar - br, None)
        elif 4 * k == n:
            even[k], odd[k] = (2.0 * ar, None), (-2.0 * ai, None)
        else:
            even[k] = (ar + br, ai - bi)
            odd[k] = turned(k, n, ar - br, ai + bi, +1)
    out = [None] * n
    out[0::2], out[1::2] = irfft(even), irfft(odd)
    return out


def halves(value):
    high = value.astype(BF16)
    return high, (value - high.astype(F32)).astype(BF16)


def toeplitz(line):
    wide = jnp.broadcast_to(line, (LANES, 2 * LANES))
    return pltpu.roll(wide, 0, 1, stride=1, stride_axis=0)[:, :LANES]


def plane_step(table_ref, src, offset, dst, extra=None):
    def step(i, _):
        pair = jnp.concatenate([src[offset + 2 * i], src[offset + 2 * i + 1]], axis=1)
        out = jnp.dot(table_ref[...], jnp.concatenate(halves(pair), axis=0), preferred_element_type=F32)
        out = out[:LANES] + out[LANES:]
        one, two = out[:, :LANES], out[:, LANES:]
        if extra is not None:
            one, two = one + extra[2 * i], two + extra[2 * i + 1]
        dst[2 * i], dst[2 * i + 1] = one, two
        return 0

    lax.fori_loop(0, 16, step, 0, unroll=2)


def kernel(
    x_hbm, row_taps, col_taps, stencil, tab_hbm, fwd_ref, inv_ref, out_hbm,
    xs, planes, got, back, sent, local, taps, my_taps, tab, lines, blocks, left, spec, prod, high, low, right,
    in_sem, out_sem, tab_sem, tap_send, tap_recv, halo_send, halo_recv, a_send, a_recv, b_send, b_recv,
):
    me = lax.axis_index("rows")

    def load(p, _):
        pltpu.make_async_copy(
            x_hbm.at[:, pl.ds(pl.multiple_of(p * LANES, LANES), LANES)], xs.at[pl.ds(1, 32), p, :], in_sem
        ).start()
        return 0

    lax.fori_loop(0, LANES, load, 0, unroll=8)
    tab_copy = pltpu.make_async_copy(tab_hbm.at[me], tab, tab_sem)
    tab_copy.start()

    barrier = pltpu.get_barrier_semaphore()

    def peer(i):
        k = (i * (i + 1) // 2) % PEERS
        core, z, x, y = k % 2, (k // 2) % 4, (k // 8) % 4, k // 32
        return (
            ((me // 32 + y) % 2 * 4 + (me // 8 + x) % 4) * 4 + (me // 2 + z) % 4
        ) * 2 + (me + core) % 2

    def greet(i, _):
        pl.semaphore_signal(barrier, inc=1, device_id={"rows": (me + i) % PEERS}, device_id_type=MESH)
        return 0

    lax.fori_loop(1, PEERS, greet, 0)

    my_taps[0:1, :] = row_taps[0:128].reshape(1, LANES)
    my_taps[1:2, :] = row_taps[128:256].reshape(1, LANES)
    padded = jnp.concatenate([col_taps[...].reshape(1, 32), jnp.zeros((1, 96), F32)], axis=1)
    my_taps[2:3, :] = pltpu.roll(padded, (me % 4) * 32, 1)
    my_taps[3:4, :] = jnp.zeros((1, LANES), F32)

    pltpu.make_async_copy(xs.at[pl.ds(1, 32)], xs.at[pl.ds(1, 32)], in_sem).wait()
    plane_step(fwd_ref, xs, 1, planes)
    pl.semaphore_wait(barrier, PEERS - 1)

    def remote(src, dst, send, recv, to):
        return pltpu.make_async_remote_copy(
            src_ref=src, dst_ref=dst, send_sem=send, recv_sem=recv, device_id={"rows": to}, device_id_type=MESH
        )

    def send_taps(i, _):
        remote(my_taps, taps.at[pl.ds(pl.multiple_of(me * 4, 4), 4), :], tap_send, tap_recv, peer(i)).start()
        return 0

    lax.fori_loop(1, PEERS, send_taps, 0)
    down = remote(xs.at[32], xs.at[0], halo_send.at[0], halo_recv.at[0], (me + 1) % PEERS)
    up = remote(xs.at[1], xs.at[33], halo_send.at[1], halo_recv.at[1], (me + PEERS - 1) % PEERS)
    down.start()
    up.start()

    for c in range(2):

        def send_plane(i, _):
            to = peer(i)
            remote(
                planes.at[:, 2 * to + c, :],
                got.at[c, pl.ds(pl.multiple_of(me * 32, 32), 32)],
                a_send.at[c],
                a_recv.at[c],
                to,
            ).start()
            return 0

        lax.fori_loop(1, PEERS, send_plane, 0)

    for c in range(2):

        def own(r, _):
            got[c, pl.ds(me * 32 + r, 1), :] = planes[r, pl.ds(2 * me + c, 1), :]
            return 0

        lax.fori_loop(0, 32, own, 0)

    taps[pl.ds(pl.multiple_of(me * 4, 4), 4), :] = my_taps[...]
    tab_copy.wait()
    pltpu.make_async_copy(taps.at[pl.ds(0, 252)], taps.at[pl.ds(0, 252)], tap_recv).wait()
    g = jnp.dot(tab[...], taps[...], preferred_element_type=F32, precision=lax.Precision.HIGHEST)
    gr, gi, hr, hi = g[0:1], g[1:2], g[2:3], g[3:4]
    wr, wi, vr, vi = (tab[i : i + 1, 0:LANES] for i in (4, 5, 6, 7))
    real = toeplitz(jnp.concatenate([gr, wr * gr - wi * gi], axis=1))
    imag = toeplitz(jnp.concatenate([gi, wr * gi + wi * gr], axis=1))
    real_two = toeplitz(jnp.concatenate([hr, vr * hr - vi * hi], axis=1))
    for r, c, value in ((0, 0, real), (0, 1, imag), (1, 0, -imag), (1, 1, real_two)):
        rows, cols = pl.ds(r * LANES, LANES), c * LANES
        h, l = halves(value)
        right[rows, cols : cols + LANES] = h
        right[rows, 256 + cols : 256 + cols + LANES] = l

    lines[...] = sum(taps[pl.ds(4 * e + 2, BLOCKS, stride=16), :] for e in range(4))

    def block(d, _):
        line = jnp.concatenate([lines[pl.ds(d, 1), :], lines[pl.ds((d + BLOCKS - 1) % BLOCKS, 1), :]], axis=1)
        blocks[d] = toeplitz(line).T
        return 0

    lax.fori_loop(0, BLOCKS, block, 0)

    def block_spectrum(t, _):
        rows = pl.ds(pl.multiple_of(t * 16, 16), 16)
        freqs = rfft([blocks[d, rows, :] for d in range(BLOCKS)])
        zero = jnp.zeros((16, LANES), F32)
        for f in range(8):
            if f == 0:
                quads = ((freqs[0][0], zero), (zero, freqs[8][0]))
            else:
                quads = ((freqs[f][0], -freqs[f][1]), (freqs[f][1], freqs[f][0]))
            for r in range(2):
                for c in range(2):
                    h, l = halves(quads[r][c] * (1.0 / BLOCKS))
                    cols = slice(c * LANES, (c + 1) * LANES)
                    left[f, pl.ds(pl.multiple_of(r * LANES + t * 16, 16), 16), cols] = h
                    left[f, pl.ds(pl.multiple_of(256 + r * LANES + t * 16, 16), 16), cols] = l
        return 0

    lax.fori_loop(0, 8, block_spectrum, 0)

    down.wait()
    up.wait()
    lane = lax.broadcasted_iota(jnp.int32, (LANES, LANES), 1)

    def stencil_row(y, _):
        total = jnp.zeros((LANES, LANES), F32)
        for a in range(3):
            here = xs[y + a]
            before, after = pltpu.roll(here, 1, 1), pltpu.roll(here, LANES - 1, 1)
            before = jnp.where(lane == 0, pltpu.roll(before, 1, 0), before)
            after = jnp.where(lane == LANES - 1, pltpu.roll(after, LANES - 1, 0), after)
            total = total + stencil[a, 0] * before + stencil[a, 1] * here + stencil[a, 2] * after
        local[y] = total
        return 0

    lax.fori_loop(0, 32, stencil_row, 0)

    for c in range(2):
        pltpu.make_async_copy(got.at[c, pl.ds(0, 2016)], got.at[c, pl.ds(0, 2016)], a_recv.at[c]).wait()

        def spectrum(t, _):
            freqs = rfft(
                [got[c, pl.ds(pl.multiple_of(b * LANES + t * 16, 16), 16), :] for b in range(BLOCKS)]
            )
            for f in range(8):
                pair = (freqs[0][0], freqs[8][0]) if f == 0 else freqs[f]
                for r in range(2):
                    h, l = halves(pair[r])
                    rows = pl.ds(pl.multiple_of(r * LANES + t * 16, 16), 16)
                    spec[f, rows, 0:LANES] = h
                    spec[f, rows, LANES : 2 * LANES] = l
            return 0

        lax.fori_loop(0, 8, spectrum, 0)

        def multiply(f, _):
            out = jnp.dot(left[f], spec[f], preferred_element_type=F32)
            out = out[:256] + out[256:]
            prod[f] = out[:, :LANES] + out[:, LANES:]
            return 0

        lax.fori_loop(0, 8, multiply, 0)

        def unspectrum(t, _):
            freqs = []
            for f in range(9):
                re = prod[f % 8, pl.ds(pl.multiple_of((f // 8) * LANES + t * 16, 16), 16), :]
                im = None
                if f % 8:
                    im = prod[f, pl.ds(pl.multiple_of(LANES + t * 16, 16), 16), :]
                freqs.append((re, im))
            for b, value in enumerate(irfft(freqs)):
                rows = pl.ds(pl.multiple_of(b * LANES + t * 16, 16), 16)
                high[rows, c * LANES : (c + 1) * LANES], low[rows, c * LANES : (c + 1) * LANES] = halves(value)
            return 0

        lax.fori_loop(0, 8, unspectrum, 0)

    def product(owners):
        rows = [pl.ds(pl.multiple_of(t * 32, 32), 32) for t in owners]
        hs = jnp.concatenate([high[r, :] for r in rows], axis=0)
        ls = jnp.concatenate([low[r, :] for r in rows], axis=0)
        return (
            jnp.dot(hs, right[:, 0:256], preferred_element_type=F32)
            + jnp.dot(hs, right[:, 256:512], preferred_element_type=F32)
            + jnp.dot(ls, right[:, 0:256], preferred_element_type=F32)
        )

    def send_back(j, _):
        owners = [peer(j * GROUP + 1 + k) for k in range(GROUP)]
        out = product(owners)
        for k, to in enumerate(owners):
            rows = pl.ds(pl.multiple_of(to * 32, 32), 32)
            for c in range(2):
                sent[c, rows, :] = out[k * 32 : (k + 1) * 32, c * LANES : (c + 1) * LANES]
                remote(sent.at[c, rows], back.at[:, 2 * me + c, :], b_send, b_recv, to).start()
        return 0

    lax.fori_loop(0, (PEERS - 1) // GROUP, send_back, 0)
    mine = product([me])
    for c in range(2):
        for r in range(32):
            back[r, pl.ds(2 * me + c, 1), :] = mine[r : r + 1, c * LANES : (c + 1) * LANES]

    for c in range(2):
        pltpu.make_async_copy(got.at[c, pl.ds(0, 2016)], got.at[c, pl.ds(0, 2016)], a_send.at[c]).wait()
    pltpu.make_async_copy(taps.at[pl.ds(0, 252)], taps.at[pl.ds(0, 252)], tap_send).wait()
    pltpu.make_async_copy(back.at[:, pl.ds(0, 126)], back.at[:, pl.ds(0, 126)], b_recv).wait()
    plane_step(inv_ref, back, 0, planes, local)

    def store(p, _):
        pltpu.make_async_copy(
            planes.at[:, p, :], out_hbm.at[:, pl.ds(pl.multiple_of(p * LANES, LANES), LANES)], out_sem
        ).start()
        return 0

    lax.fori_loop(0, LANES, store, 0, unroll=8)
    pltpu.make_async_copy(back.at[:, pl.ds(0, 126)], back.at[:, pl.ds(0, 126)], b_send).wait()
    pltpu.make_async_copy(planes, planes, out_sem).wait()


def body(pixels, row_taps, column_taps, stencil):
    fwd, inv = plane_tables()
    vmem, anywhere = pl.BlockSpec(memory_space=pltpu.VMEM), pl.BlockSpec(memory_space=pl.ANY)
    block = (32, LANES, LANES)
    dma = pltpu.SemaphoreType.DMA
    return pl.pallas_call(
        kernel,
        out_shape=jax.ShapeDtypeStruct(pixels.shape, F32),
        in_specs=[
            anywhere, vmem, vmem, pl.BlockSpec(memory_space=pltpu.SMEM), anywhere, vmem, vmem,
        ],
        out_specs=anywhere,
        scratch_shapes=[
            pltpu.VMEM((34, LANES, LANES), F32),
            pltpu.VMEM(block, F32),
            pltpu.VMEM((2, 2048, LANES), F32),
            pltpu.VMEM(block, F32),
            pltpu.VMEM((2, 2048, LANES), F32),
            pltpu.VMEM(block, F32),
            pltpu.VMEM((4 * PEERS, LANES), F32),
            pltpu.VMEM((4, LANES), F32),
            pltpu.VMEM((8, 2 * LANES), F32),
            pltpu.VMEM((BLOCKS, LANES), F32),
            pltpu.VMEM((BLOCKS, LANES, LANES), F32),
            pltpu.VMEM((8, 512, 256), BF16),
            pltpu.VMEM((8, 256, 256), BF16),
            pltpu.VMEM((8, 256, LANES), F32),
            pltpu.VMEM((2048, 256), BF16),
            pltpu.VMEM((2048, 256), BF16),
            pltpu.VMEM((256, 512), BF16),
            dma, dma, dma, dma, dma, dma((2,)), dma((2,)), dma((2,)), dma((2,)), dma, dma,
        ],
        compiler_params=pltpu.CompilerParams(
            collective_id=0, has_side_effects=True, vmem_limit_bytes=48 * 2**20
        ),
        name="filter_rows_and_columns",
    )(pixels, row_taps, column_taps, stencil, jnp.asarray(tap_tables()), jnp.asarray(fwd), jnp.asarray(inv))


def solution(mesh):
    in_specs = (
        P(("chan", "rows"), None),
        P(("chan", "rows")),
        P(("chan", "rows")),
        P("chan", None),
    )
    return jax.shard_map(
        body, mesh=mesh, in_specs=in_specs, out_specs=P(("chan", "rows"), None), check_vma=False
    )
```

time: 266 us -> 83.3 us (0.31); the launches traced: 261 us -> 83.1 us
  Pallas kernels: 0 us -> 75.3 us
  local copies, waits for them, and re-layouts: 80.5 us -> 7.77 us
  matrix products: 69.8 us -> 0 us
  waiting for transfers between devices: 49.9 us -> 0 us
  starting transfers between devices: 33 us -> 0 us
  other arithmetic: 27.4 us -> 0 us
    pallas_call x0 -> x1, Pallas kernels: none -> 75.3 us  [body(): pl.pallas_call(kernel, out_shape=jax.ShapeDtypeStruct(pixels.shape, F32),...]
    dot_general x36 -> x0, matrix products: 69.8 us -> none  [contract(): jnp.einsum(form, left, right, precision=dft_precision, preferred_element_...]
    all_to_all x4 -> x0, waiting for transfers between devices: 49.9 us -> none  [the longest x1 23.1 us: body(): lax.all_to_all(convolve(shaped, column_filter, column_tables, column_form...]
    all_to_all x4 -> x0, starting transfers between devices: 31.3 us -> none  [the longest x2 20.1 us: from_everyone(): lax.all_to_all(jnp.broadcast_to(shard[None], (count, *shard.shape)), axis...]
    unnamed x22 -> x15, local copies, waits for them, and re-layouts: 24.8 us -> 7.77 us
    all_to_all x4 -> x0, local copies, waits for them, and re-layouts: 15.3 us -> none  [the longest x2 12.2 us: body(): lax.all_to_all(blocks, 'rows', split_axis=2, concat_axis=0, tiled=True)]
    another operation x2 -> x0, local copies, waits for them, and re-layouts: 15.2 us -> none  [body(): blocks = convolve(shaped, row_filter, row_tables, row_forms).reshape(pixe...]
    add x1 -> x0, other arithmetic: 13.3 us -> none  [body(): filtered + stencil[offset_row, offset_col] * jnp.roll(row_band, 1 - offse...]
  transfers between devices with their start and end apart: 6 -> 0, of which waited for: 3 -> 0; matrix products, arithmetic and copies ran while one was open for 34% -> 0% of each run, Pallas kernels for 0% -> 0%
where the time goes in v1:
time: 83.3 us; the launch traced here: 83.1 us
  Pallas kernels  75.3 us (90%)
  local copies, waits for them, and re-layouts  7.77 us (9%)
    pallas_call x1, Pallas kernels, body(): pl.pallas_call(kernel, out_shape=jax.ShapeDtypeStruct(pixels.shape, F32),...  75.3 us
    unnamed x15, local copies, waits for them, and re-layouts  7.77 us

profile of v1, /device:TPU:1, one launch (start us, length us, event | category | flops | bytes accessed | tf_op | source)
XLA Modules:
  0.0 83.1 jit_solution(14999848745413108877)
XLA Ops:
  0.0 0.0 copy-start
  0.0 1.6 %copy-done = f32[32,16384]{1,0:T(8,128)S(1)} copy-done((f32[32,16384]{1,0:T(8,128)S(1)}, f32[32,16384]{1,0:T(8,128)}, u32[]{:S(2)}) %copy-start) | copy-done | bytes 2097176
  1.6 0.0 copy-start.1
  1.6 1.0 %copy-done.1 = f32[64,8,256]{2,1,0:T(8,128)S(1)} copy-done((f32[64,8,256]{2,1,0:T(8,128)S(1)}, f32[64,8,256]{2,1,0:T(8,128)}, u32[]{:S(2)}) %copy-start.1) | copy-done | bytes 524312
  2.6 0.0 copy-start.2
  2.6 0.9 %copy-done.2 = bf16[256,256]{1,0:T(8,128)(2,1)S(1)} copy-done((bf16[256,256]{1,0:T(8,128)(2,1)S(1)}, bf16[256,256]{1,0:T(8,128)(2,1)}, u32[]{:S(2)}) %copy-start.2) | copy-done | bytes 131096
  3.5 0.0 copy-start.3
  3.5 0.9 %copy-done.3 = bf16[256,256]{1,0:T(8,128)(2,1)S(1)} copy-done((bf16[256,256]{1,0:T(8,128)(2,1)S(1)}, bf16[256,256]{1,0:T(8,128)(2,1)}, u32[]{:S(2)}) %copy-start.3) | copy-done | bytes 131096
  4.4 0.0 copy-start.4
  4.4 0.7 copy-done.4
  5.1 0.0 copy-start.5
  5.1 0.7 copy-done.5
  5.8 0.0 copy-start.6
  5.8 0.7 copy-done.6
  6.5 75.3 %filter_rows_and_columns.1 = f32[32,16384]{1,0:T(8,128)S(1)} custom-call(f32[32,16384]{1,0:T(8,128)S(1)} %copy-done, f32[256]{0:T(256)S(1)} %copy-done.5, f32[32]{0:T(128)S(1)} %copy-done.6, f32[3,3]{1,0:T(4,128)S(1)} %copy-done.4, f32[64,8,256]{2,1,0:T(8,128)S(1)} %copy-done.1, bf16[256,256]{1,0:T(8,128)(2,1)S(1)} %copy-done.3, bf16[256,256]{1,0:T(8,128)(2,1)S(1)} %copy-done.2), custom_call_target="tpu_custom_call" | custom-call | tf_op jit(solution)/shard_map/filter_rows_and_columns/pallas_call | solution.py:365
  81.8 1.3 %copy.9 = f32[32,16384]{1,0:T(8,128)} copy(f32[32,16384]{1,0:T(8,128)S(1)} %filter_rows_and_columns.1) | data formatting | bytes 4194304
Async XLA Ops:
  0.0 1.6 %copy-start = (f32[32,16384]{1,0:T(8,128)S(1)}, f32[32,16384]{1,0:T(8,128)}, u32[]{:S(2)}) copy-start(f32[32,16384]{1,0:T(8,128)} %x_hbm.1) | copy-start | bytes 6291460
  1.6 1.0 %copy-start.1 = (f32[64,8,256]{2,1,0:T(8,128)S(1)}, f32[64,8,256]{2,1,0:T(8,128)}, u32[]{:S(2)}) copy-start(f32[64,8,256]{2,1,0:T(8,128)} %constant.6.clone.tab_hbm) | copy-start | bytes 1572868
  2.6 0.9 %copy-start.2 = (bf16[256,256]{1,0:T(8,128)(2,1)S(1)}, bf16[256,256]{1,0:T(8,128)(2,1)}, u32[]{:S(2)}) copy-start(bf16[256,256]{1,0:T(8,128)(2,1)} %constant.8.clone.inv_ref) | copy-start | bytes 393220
  3.5 0.9 %copy-start.3 = (bf16[256,256]{1,0:T(8,128)(2,1)S(1)}, bf16[256,256]{1,0:T(8,128)(2,1)}, u32[]{:S(2)}) copy-start(bf16[256,256]{1,0:T(8,128)(2,1)} %constant.7.clone.fwd_ref) | copy-start | bytes 393220
  4.4 0.7 copy-start.4
  5.1 0.7 copy-start.5
  5.8 0.7 copy-start.6

commit v2 on v1

v2 whole, which is shorter than its diff:
```python
import math

import jax
import jax.numpy as jnp
import ml_dtypes
import numpy as np
from jax import lax
from jax.experimental import pallas as pl
from jax.experimental.pallas import tpu as pltpu
from jax.sharding import PartitionSpec as P

MESH = pl.DeviceIdType.MESH
F32, BF16 = jnp.float32, jnp.bfloat16
PEERS = 64
LANES = 128
BLOCKS = 16
GROUP = 7


def split_np(values):
    high = values.astype(ml_dtypes.bfloat16)
    low = (values - high.astype(np.float64)).astype(ml_dtypes.bfloat16)
    return high, low


def frequency(device, phase):
    return LANES // 2 if device == 1 and phase == 0 else 2 * (device // 2) + phase


def plane_tables():
    pos = np.arange(LANES)
    fwd = np.zeros((2, PEERS, LANES))
    inv = np.zeros((2, LANES, PEERS))
    for phase in range(2):
        for device in range(PEERS):
            freq = frequency(device, phase)
            angle = 2 * np.pi * (pos * freq % LANES) / LANES
            real = freq in (0, LANES // 2)
            wave = -np.sin(angle) if device % 2 and not real else np.cos(angle)
            fwd[phase, device] = wave
            inv[phase, :, device] = wave * (1 if real else 2) / LANES
    high, low = split_np(fwd.reshape(LANES, LANES))
    forward = np.block([[high, high], [low, low]])
    high, low = split_np(inv)
    return forward, np.concatenate([high, high, low], axis=2)


def tap_tables():
    tab = np.zeros((PEERS, 8, 2 * LANES), np.float64)
    pos = np.arange(LANES)
    cols = pos // 2 % 2 * LANES + pos // 4 * 4 + pos % 2
    for device in range(PEERS):
        for phase in range(2):
            freq = frequency(device, phase)
            angle = 2 * np.pi * (pos * freq % LANES) / LANES
            tab[device, 2 * phase, cols], tab[device, 2 * phase + 1, cols] = np.cos(angle), -np.sin(angle)
            turn = 2 * np.pi * freq / LANES
            tab[device, 4 + 2 * phase], tab[device, 5 + 2 * phase] = np.cos(turn), -np.sin(turn)
    return tab.astype(np.float32)


def turned(k, n, re, im, sign):
    angle = 2 * math.pi * k / n
    c, s = math.cos(angle), sign * math.sin(angle)
    if k == 0:
        return re, im
    if 4 * k == n:
        return (-im, re) if sign > 0 else (im, -re)
    if 8 * k == n:
        return (re - s / abs(s) * im) * c, (im + s / abs(s) * re) * c
    return re * c - im * s, re * s + im * c


def rfft(values):
    n = len(values)
    if n == 2:
        return [(values[0] + values[1], None), (values[0] - values[1], None)]
    even, odd = rfft(values[0::2]), rfft(values[1::2])
    out = [None] * (n // 2 + 1)
    for k in range(n // 4 + 1):
        er, ei = even[k]
        orr, oi = odd[k]
        if k == 0:
            out[0], out[n // 2] = (er + orr, None), (er - orr, None)
        elif 4 * k == n:
            out[k] = (er, -orr)
        else:
            tr, ti = turned(k, n, orr, oi, -1)
            out[k] = (er + tr, ei + ti)
            out[n // 2 - k] = (er - tr, ti - ei)
    return out


def irfft(spectrum):
    n = 2 * (len(spectrum) - 1)
    if n == 2:
        a, b = spectrum[0][0], spectrum[1][0]
        return [a + b, a - b]
    even, odd = [None] * (n // 4 + 1), [None] * (n // 4 + 1)
    for k in range(n // 4 + 1):
        ar, ai = spectrum[k]
        br, bi = spectrum[n // 2 - k]
        if k == 0:
            even[0], odd[0] = (ar + br, None), (ar - br, None)
        elif 4 * k == n:
            even[k], odd[k] = (2.0 * ar, None), (-2.0 * ai, None)
        else:
            even[k] = (ar + br, ai - bi)
            odd[k] = turned(k, n, ar - br, ai + bi, +1)
    out = [None] * n
    out[0::2], out[1::2] = irfft(even), irfft(odd)
    return out


def halves(value):
    high = value.astype(BF16)
    return high, (value - high.astype(F32)).astype(BF16)


def toeplitz(line):
    wide = jnp.broadcast_to(line, (LANES, 2 * LANES))
    return pltpu.roll(wide, 0, 1, stride=1, stride_axis=0)[:, :LANES]


def kernel(
    x_hbm, row_taps_hbm, col_taps_hbm, stencil_hbm, tab_hbm, fwd_hbm, inv_hbm, out_hbm,
    row_taps, col_taps, stencil, fwd_ref, inv_ref, tab, my_taps, taps,
    xs, planes, got, done, other, sent, back, local, lines, blocks, left, spec, prod, right,
    in_sem, out_sem, small_sems, tap_send, tap_recv, share_send, share_recv, halo_send, halo_recv,
    a_send, a_recv, swap_send, swap_recv, b_send, b_recv,
):
    me = lax.axis_index("rows")
    core, chip = me % 2, me // 2
    sibling = chip * 2 + 1 - core

    def load(p, _):
        pltpu.make_async_copy(
            x_hbm.at[:, pl.ds(pl.multiple_of(p * LANES, LANES), LANES)], xs.at[pl.ds(1, 32), p, :], in_sem
        ).start()
        return 0

    lax.fori_loop(0, LANES, load, 0, unroll=8)
    pairs = (
        (row_taps_hbm, row_taps), (col_taps_hbm, col_taps), (stencil_hbm, stencil), (fwd_hbm, fwd_ref),
        (tab_hbm.at[me], tab), (inv_hbm, inv_ref),
    )
    small = [pltpu.make_async_copy(src, dst, small_sems.at[i]) for i, (src, dst) in enumerate(pairs)]
    for copy in small:
        copy.start()

    barrier = pltpu.get_barrier_semaphore()

    def away(k):
        return (
            ((me // 32 + k // 32) % 2 * 4 + (me // 8 + k // 8 % 4) % 4) * 4 + (me // 2 + k // 2 % 4) % 4
        ) * 2 + (me + k % 2) % 2

    def peer(i):
        return away((i * (i + 1) // 2) % PEERS)

    def greet(i, _):
        pl.semaphore_signal(barrier, inc=1, device_id={"rows": (me + i) % PEERS}, device_id_type=MESH)
        return 0

    lax.fori_loop(1, PEERS, greet, 0)

    small[0].wait()
    small[1].wait()
    my_taps[0:1, :] = row_taps[0:128].reshape(1, LANES)
    my_taps[1:2, :] = row_taps[128:256].reshape(1, LANES)
    padded = jnp.concatenate([col_taps[...].reshape(1, 32), jnp.zeros((1, 96), F32)], axis=1)
    my_taps[2:3, :] = pltpu.roll(padded, (me % 4) * 32, 1)
    my_taps[3:4, :] = jnp.zeros((1, LANES), F32)
    my_tap_rows = pl.ds(pl.multiple_of(chip * 4, 4), 4)
    taps[core, my_tap_rows, :] = my_taps[...]

    small[3].wait()
    pltpu.make_async_copy(xs.at[pl.ds(1, 32)], xs.at[pl.ds(1, 32)], in_sem).wait()

    def to_planes(i, _):
        pair = jnp.concatenate([xs[2 * i + 1], xs[2 * i + 2]], axis=1)
        out = jnp.dot(fwd_ref[...], jnp.concatenate(halves(pair), axis=0), preferred_element_type=F32)
        out = out[:LANES] + out[LANES:]
        for f in range(2):
            for r in range(2):
                planes[f, 2 * i + r] = out[f * PEERS : (f + 1) * PEERS, r * LANES : (r + 1) * LANES]
        return 0

    lax.fori_loop(0, 16, to_planes, 0, unroll=2)
    pl.semaphore_wait(barrier, PEERS - 1)

    def remote(src, dst, send, recv, to):
        return pltpu.make_async_remote_copy(
            src_ref=src, dst_ref=dst, send_sem=send, recv_sem=recv, device_id={"rows": to}, device_id_type=MESH
        )

    def send_taps(i, _):
        to = away((i * (i + 1) // 2) % 32 * 2)
        remote(my_taps, taps.at[core, my_tap_rows, :], tap_send, tap_recv, to).start()
        return 0

    lax.fori_loop(1, 32, send_taps, 0)

    for f in range(2):

        def send_plane(i, _):
            to = peer(i)
            remote(
                planes.at[f, :, to, :],
                got.at[f, pl.ds(pl.multiple_of(me * 32, 32), 32)],
                a_send.at[f],
                a_recv.at[f],
                to,
            ).start()
            return 0

        lax.fori_loop(1, PEERS, send_plane, 0)

    down = remote(xs.at[32], xs.at[0], halo_send.at[0], halo_recv.at[0], (me + 1) % PEERS)
    up = remote(xs.at[1], xs.at[33], halo_send.at[1], halo_recv.at[1], (me + PEERS - 1) % PEERS)
    down.start()
    up.start()

    for f in range(2):

        def own(r, _):
            got[f, pl.ds(me * 32 + r, 1), :] = planes[f, r, pl.ds(me, 1), :]
            return 0

        lax.fori_loop(0, 32, own, 0)

    small[4].wait()
    pltpu.make_async_copy(taps.at[0, pl.ds(0, 124)], taps.at[0, pl.ds(0, 124)], tap_recv).wait()
    share = remote(taps.at[core], taps.at[core], share_send, share_recv, sibling)
    share.start()
    share.wait()
    g = jnp.dot(tab[:, 0:LANES], taps[0], preferred_element_type=F32, precision=lax.Precision.HIGHEST)
    g = g + jnp.dot(tab[:, LANES:], taps[1], preferred_element_type=F32, precision=lax.Precision.HIGHEST)
    sign = (2 * core - 1).astype(F32)
    for f in range(2):
        gr, gi = g[2 * f : 2 * f + 1], g[2 * f + 1 : 2 * f + 2]
        wr, wi = tab[4 + 2 * f : 5 + 2 * f, 0:LANES], tab[5 + 2 * f : 6 + 2 * f, 0:LANES]
        same = toeplitz(jnp.concatenate([gr, wr * gr - wi * gi], axis=1))
        cross = toeplitz(jnp.concatenate([gi, wr * gi + wi * gr], axis=1) * sign)
        for r, value in enumerate((same, cross)):
            h, l = halves(value)
            right[f, r * LANES : (r + 1) * LANES, 0:LANES] = h
            right[f, r * LANES : (r + 1) * LANES, LANES : 2 * LANES] = l

    lines[...] = sum(taps[c, pl.ds(4 * e + 2, BLOCKS, stride=8), :] for e in range(2) for c in range(2))

    def block(d, _):
        line = jnp.concatenate([lines[pl.ds(d, 1), :], lines[pl.ds((d + BLOCKS - 1) % BLOCKS, 1), :]], axis=1)
        blocks[d] = toeplitz(line).T
        return 0

    lax.fori_loop(0, BLOCKS, block, 0)

    def block_spectrum(t, _):
        rows = pl.ds(pl.multiple_of(t * 16, 16), 16)
        freqs = rfft([blocks[d, rows, :] for d in range(BLOCKS)])
        zero = jnp.zeros((16, LANES), F32)
        for f in range(8):
            if f == 0:
                quads = ((freqs[0][0], zero), (zero, freqs[8][0]))
            else:
                quads = ((freqs[f][0], -freqs[f][1]), (freqs[f][1], freqs[f][0]))
            for r in range(2):
                for c in range(2):
                    h, l = halves(quads[r][c] * (1.0 / BLOCKS))
                    cols = slice(c * LANES, (c + 1) * LANES)
                    left[f, pl.ds(pl.multiple_of(r * LANES + t * 16, 16), 16), cols] = h
                    left[f, pl.ds(pl.multiple_of(256 + r * LANES + t * 16, 16), 16), cols] = l
        return 0

    lax.fori_loop(0, 8, block_spectrum, 0)

    for f in range(2):
        pltpu.make_async_copy(got.at[f, pl.ds(0, 2016)], got.at[f, pl.ds(0, 2016)], a_recv.at[f]).wait()

        def spectrum(t, _):
            freqs = rfft(
                [got[f, pl.ds(pl.multiple_of(b * LANES + t * 16, 16), 16), :] for b in range(BLOCKS)]
            )
            for k in range(8):
                pair = (freqs[0][0], freqs[8][0]) if k == 0 else freqs[k]
                for r in range(2):
                    h, l = halves(pair[r])
                    rows = pl.ds(pl.multiple_of(r * LANES + t * 16, 16), 16)
                    spec[k, rows, 0:LANES] = h
                    spec[k, rows, LANES : 2 * LANES] = l
            return 0

        lax.fori_loop(0, 8, spectrum, 0)

        def multiply(k, _):
            out = jnp.dot(left[k], spec[k], preferred_element_type=F32)
            out = out[:256] + out[256:]
            prod[k] = out[:, :LANES] + out[:, LANES:]
            return 0

        lax.fori_loop(0, 8, multiply, 0)

        def unspectrum(t, _):
            freqs = []
            for k in range(9):
                re = prod[k % 8, pl.ds(pl.multiple_of((k // 8) * LANES + t * 16, 16), 16), :]
                im = None
                if k % 8:
                    im = prod[k, pl.ds(pl.multiple_of(LANES + t * 16, 16), 16), :]
                freqs.append((re, im))
            for b, value in enumerate(irfft(freqs)):
                done[f, pl.ds(pl.multiple_of(b * LANES + t * 16, 16), 16), :] = value
            return 0

        lax.fori_loop(0, 8, unspectrum, 0)
        swap = remote(done.at[f], other.at[f], swap_send.at[f], swap_recv.at[f], sibling)
        swap.start()
        swap.wait()

        def product(owners):
            rows = [pl.ds(pl.multiple_of(t * 32, 32), 32) for t in owners]
            both = [
                jnp.concatenate([ref[f, r, :] for r in rows], axis=0) for ref in (done, other)
            ]
            h, l = halves(jnp.concatenate(both, axis=1))
            out = jnp.dot(h, right[f], preferred_element_type=F32)
            return out[:, :LANES] + out[:, LANES:] + jnp.dot(l, right[f, :, 0:LANES], preferred_element_type=F32)

        def send_back(j, _):
            owners = [peer(j * GROUP + 1 + k) for k in range(GROUP)]
            out = product(owners)
            for k, to in enumerate(owners):
                rows = pl.ds(pl.multiple_of(to * 32, 32), 32)
                sent[f, rows, :] = out[k * 32 : (k + 1) * 32]
                remote(sent.at[f, rows], back.at[f, :, me, :], b_send.at[f], b_recv.at[f], to).start()
            return 0

        lax.fori_loop(0, (PEERS - 1) // GROUP, send_back, 0)
        mine = product([me])
        for r in range(32):
            back[f, r, pl.ds(me, 1), :] = mine[r : r + 1]

    small[2].wait()
    small[5].wait()
    down.wait()
    up.wait()
    lane = lax.broadcasted_iota(jnp.int32, (LANES, LANES), 1)

    def stencil_row(y, _):
        total = jnp.zeros((LANES, LANES), F32)
        for a in range(3):
            here = xs[y + a]
            before, after = pltpu.roll(here, 1, 1), pltpu.roll(here, LANES - 1, 1)
            before = jnp.where(lane == 0, pltpu.roll(before, 1, 0), before)
            after = jnp.where(lane == LANES - 1, pltpu.roll(after, LANES - 1, 0), after)
            total = total + stencil[a, 0] * before + stencil[a, 1] * here + stencil[a, 2] * after
        local[y] = total
        return 0

    lax.fori_loop(0, 32, stencil_row, 0)

    for f in range(2):
        pltpu.make_async_copy(got.at[f, pl.ds(0, 2016)], got.at[f, pl.ds(0, 2016)], a_send.at[f]).wait()
    pltpu.make_async_copy(taps.at[0, pl.ds(0, 124)], taps.at[0, pl.ds(0, 124)], tap_send).wait()

    for f in range(2):
        pltpu.make_async_copy(got.at[f, pl.ds(0, 2016)], got.at[f, pl.ds(0, 2016)], b_recv.at[f]).wait()

        def from_planes(i, _):
            pair = jnp.concatenate([back[f, 2 * i], back[f, 2 * i + 1]], axis=1)
            h, l = halves(pair)
            out = jnp.dot(inv_ref[f], jnp.concatenate([h, l, h], axis=0), preferred_element_type=F32)
            local[2 * i] += out[:, :LANES]
            local[2 * i + 1] += out[:, LANES:]
            return 0

        lax.fori_loop(0, 16, from_planes, 0, unroll=2)

    def store(p, _):
        pltpu.make_async_copy(
            local.at[:, p, :], out_hbm.at[:, pl.ds(pl.multiple_of(p * LANES, LANES), LANES)], out_sem
        ).start()
        return 0

    lax.fori_loop(0, LANES, store, 0, unroll=8)
    for f in range(2):
        pltpu.make_async_copy(got.at[f, pl.ds(0, 2016)], got.at[f, pl.ds(0, 2016)], b_send.at[f]).wait()
    pltpu.make_async_copy(local, local, out_sem).wait()


def body(pixels, row_taps, column_taps, stencil):
    fwd, inv = plane_tables()
    hbm = pl.BlockSpec(memory_space=pltpu.HBM)
    block = (32, LANES, LANES)
    columns = (2, 2048, LANES)
    dma = pltpu.SemaphoreType.DMA
    return pl.pallas_call(
        kernel,
        out_shape=jax.ShapeDtypeStruct(pixels.shape, F32),
        in_specs=[hbm] * 7,
        out_specs=hbm,
        scratch_shapes=[
            pltpu.VMEM((256,), F32),
            pltpu.VMEM((32,), F32),
            pltpu.SMEM((3, 3), F32),
            pltpu.VMEM((256, 256), BF16),
            pltpu.VMEM((2, LANES, 192), BF16),
            pltpu.VMEM((8, 2 * LANES), F32),
            pltpu.VMEM((4, LANES), F32),
            pltpu.VMEM((2, LANES, LANES), F32),
            pltpu.VMEM((34, LANES, LANES), F32),
            pltpu.VMEM((2, 32, PEERS, LANES), F32),
            pltpu.VMEM(columns, F32),
            pltpu.VMEM(columns, F32),
            pltpu.VMEM(columns, F32),
            pltpu.VMEM(columns, F32),
            pltpu.VMEM((2, 32, PEERS, LANES), F32),
            pltpu.VMEM(block, F32),
            pltpu.VMEM((BLOCKS, LANES), F32),
            pltpu.VMEM((BLOCKS, LANES, LANES), F32),
            pltpu.VMEM((8, 512, 256), BF16),
            pltpu.VMEM((8, 256, 256), BF16),
            pltpu.VMEM((8, 256, LANES), F32),
            pltpu.VMEM((2, 256, 256), BF16),
            dma, dma, dma((6,)), dma, dma, dma, dma, dma((2,)), dma((2,)),
            dma((2,)), dma((2,)), dma((2,)), dma((2,)), dma((2,)), dma((2,)),
        ],
        compiler_params=pltpu.CompilerParams(
            collective_id=0, has_side_effects=True, vmem_limit_bytes=67_043_328
        ),
        name="filter_rows_and_columns",
    )(pixels, row_taps, column_taps, stencil, jnp.asarray(tap_tables()), jnp.asarray(fwd), jnp.asarray(inv))


def solution(mesh):
    in_specs = (
        P(("chan", "rows"), None),
        P(("chan", "rows")),
        P(("chan", "rows")),
        P("chan", None),
    )
    return jax.shard_map(
        body, mesh=mesh, in_specs=in_specs, out_specs=P(("chan", "rows"), None), check_vma=False
    )
```

time: 83.3 us -> 66.5 us (0.80)
  Pallas kernels: 75.3 us -> 63.3 us
  local copies, waits for them, and re-layouts: 7.77 us -> 3.05 us
    pallas_call x1, Pallas kernels: 75.3 us -> 63.3 us  [body(): pl.pallas_call(kernel, out_shape=jax.ShapeDtypeStruct(pixels.shape, F32),...]
    unnamed x15 -> x1, local copies, waits for them, and re-layouts: 7.77 us -> 3.05 us
where the time goes in v2:
time: 66.5 us; the launch traced here: 66.4 us
  Pallas kernels  63.3 us (95%)
  local copies, waits for them, and re-layouts  3.05 us (5%)
    pallas_call x1, Pallas kernels, body(): pl.pallas_call(kernel, out_shape=jax.ShapeDtypeStruct(pixels.shape, F32),...  63.3 us
    unnamed x1, local copies, waits for them, and re-layouts  3.05 us

profile of v2, /device:TPU:1, one launch (start us, length us, event | category | flops | bytes accessed | tf_op | source)
XLA Modules:
  0.0 66.4 jit_solution(3280766173587679819)
XLA Ops:
  0.0 63.3 %filter_rows_and_columns.1 = f32[32,16384]{1,0:T(8,128)} custom-call(f32[32,16384]{1,0:T(8,128)} %x_hbm.1, f32[256]{0:T(256)} %row_taps_hbm.1, f32[32]{0:T(128)} %col_taps_hbm.1, f32[3,3]{1,0:T(4,128)} %stencil_hbm.1, f32[64,8,256]{2,1,0:T(8,128)} %constant.6.clone.tab_hbm, bf16[256,256]{1,0:T(8,128)(2,1)} %constant.7.clone.fwd_hbm, ...), custom_call_target="tpu_custom_call" | custom-call | tf_op jit(solution)/shard_map/filter_rows_and_columns/pallas_call | solution.py:398
  63.3 3.0 %copy.9 = f32[32,16384]{1,0:T(8,128)} copy(f32[32,16384]{1,0:T(8,128)} %filter_rows_and_columns.1) | data formatting | bytes 4194304

commit v3 on v2

--- a/solution.py
+++ b/solution.py
@@ -14,7 +14,13 @@
 PEERS = 64
 LANES = 128
 BLOCKS = 16
+MAIN_LIMIT = 67_043_328
+FINISH_LIMIT = 67_043_328
+PARTS = 1
 GROUP = 7
+
+
+STEPS = [(i * (i + 1) // 2) % PEERS for i in range(1, PEERS)]
 
 
 def split_np(values):
@@ -122,15 +128,27 @@
     return pltpu.roll(wide, 0, 1, stride=1, stride_axis=0)[:, :LANES]
 
 
+def add_planes(table_ref, planes, base, total):
+    def step(i, _):
+        h, l = halves(jnp.concatenate([planes[2 * i], planes[2 * i + 1]], axis=1))
+        out = jnp.dot(table_ref[...], jnp.concatenate([h, l, h], axis=0), preferred_element_type=F32)
+        total[2 * i] = base[2 * i] + out[:, :LANES]
+        total[2 * i + 1] = base[2 * i + 1] + out[:, LANES:]
+        return 0
+
+    lax.fori_loop(0, total.shape[0] // 2, step, 0, unroll=4)
+
+
 def kernel(
-    x_hbm, row_taps_hbm, col_taps_hbm, stencil_hbm, tab_hbm, fwd_hbm, inv_hbm, out_hbm,
+    x_hbm, row_taps_hbm, col_taps_hbm, stencil_hbm, tab_hbm, fwd_hbm, inv_hbm, local_hbm, last,
     row_taps, col_taps, stencil, fwd_ref, inv_ref, tab, my_taps, taps,
-    xs, planes, got, done, other, sent, back, local, lines, blocks, left, spec, prod, right,
-    in_sem, out_sem, small_sems, tap_send, tap_recv, share_send, share_recv, halo_send, halo_recv,
+    xs, planes, got, done, other, sent, first, local, lines, blocks, left, spec, prod, right,
+    in_sem, out_sems, small_sems, tap_send, tap_recv, share_send, share_recv, halo_send, halo_recv,
     a_send, a_recv, swap_send, swap_recv, b_send, b_recv,
 ):
     me = lax.axis_index("rows")
     core, chip = me % 2, me // 2
+    back = (first, last)
     sibling = chip * 2 + 1 - core
 
     def load(p, _):
@@ -150,19 +168,14 @@
 
     barrier = pltpu.get_barrier_semaphore()
 
-    def away(k):
-        return (
-            ((me // 32 + k // 32) % 2 * 4 + (me // 8 + k // 8 % 4) % 4) * 4 + (me // 2 + k // 2 % 4) % 4
-        ) * 2 + (me + k % 2) % 2
-
-    def peer(i):
-        return away((i * (i + 1) // 2) % PEERS)
-
-    def greet(i, _):
-        pl.semaphore_signal(barrier, inc=1, device_id={"rows": (me + i) % PEERS}, device_id_type=MESH)
-        return 0
-
-    lax.fori_loop(1, PEERS, greet, 0)
+    ys = [(me // 32 + k) % 2 * 32 for k in range(2)]
+    xs_at = [(me // 8 + k) % 4 * 8 for k in range(4)]
+    zs = [(me // 2 + k) % 4 * 2 for k in range(4)]
+    cores = [(me + k) % 2 for k in range(2)]
+    peers = [ys[k // 32] + xs_at[k // 8 % 4] + zs[k // 2 % 4] + cores[k % 2] for k in STEPS]
+
+    for to in peers:
+        pl.semaphore_signal(barrier, inc=1, device_id={"rows": to}, device_id_type=MESH)
 
     small[0].wait()
     small[1].wait()
@@ -186,7 +199,7 @@
                 planes[f, 2 * i + r] = out[f * PEERS : (f + 1) * PEERS, r * LANES : (r + 1) * LANES]
         return 0
 
-    lax.fori_loop(0, 16, to_planes, 0, unroll=2)
+    lax.fori_loop(0, 16, to_planes, 0, unroll=4)
     pl.semaphore_wait(barrier, PEERS - 1)
 
     def remote(src, dst, send, recv, to):
@@ -194,17 +207,11 @@
             src_ref=src, dst_ref=dst, send_sem=send, recv_sem=recv, device_id={"rows": to}, device_id_type=MESH
         )
 
-    def send_taps(i, _):
-        to = away((i * (i + 1) // 2) % 32 * 2)
-        remote(my_taps, taps.at[core, my_tap_rows, :], tap_send, tap_recv, to).start()
-        return 0
-
-    lax.fori_loop(1, 32, send_taps, 0)
-
-    for f in range(2):
-
-        def send_plane(i, _):
-            to = peer(i)
+    for step, to in zip(STEPS, peers):
+        if step % 2 == 0:
+            remote(my_taps, taps.at[core, my_tap_rows, :], tap_send, tap_recv, to).start()
+    for f in range(2):
+        for to in peers:
             remote(
                 planes.at[f, :, to, :],
                 got.at[f, pl.ds(pl.multiple_of(me * 32, 32), 32)],
@@ -212,9 +219,6 @@
                 a_recv.at[f],
                 to,
             ).start()
-            return 0
-
-        lax.fori_loop(1, PEERS, send_plane, 0)
 
     down = remote(xs.at[32], xs.at[0], halo_send.at[0], halo_recv.at[0], (me + 1) % PEERS)
     up = remote(xs.at[1], xs.at[33], halo_send.at[1], halo_recv.at[1], (me + PEERS - 1) % PEERS)
@@ -327,19 +331,23 @@
             out = jnp.dot(h, right[f], preferred_element_type=F32)
             return out[:, :LANES] + out[:, LANES:] + jnp.dot(l, right[f, :, 0:LANES], preferred_element_type=F32)
 
-        def send_back(j, _):
-            owners = [peer(j * GROUP + 1 + k) for k in range(GROUP)]
+        for j in range(0, PEERS - 1, GROUP):
+            owners = peers[j : j + GROUP]
             out = product(owners)
             for k, to in enumerate(owners):
                 rows = pl.ds(pl.multiple_of(to * 32, 32), 32)
                 sent[f, rows, :] = out[k * 32 : (k + 1) * 32]
-                remote(sent.at[f, rows], back.at[f, :, me, :], b_send.at[f], b_recv.at[f], to).start()
-            return 0
-
-        lax.fori_loop(0, (PEERS - 1) // GROUP, send_back, 0)
+                remote(sent.at[f, rows], back[f].at[:, me, :], b_send.at[f], b_recv.at[f], to).start()
+
         mine = product([me])
-        for r in range(32):
-            back[f, r, pl.ds(me, 1), :] = mine[r : r + 1]
+        if f == 0:
+            for r in range(32):
+                first[r, pl.ds(me, 1), :] = mine[r : r + 1]
+        else:
+            rows = pl.ds(pl.multiple_of(me * 32, 32), 32)
+            sent[f, rows, :] = mine
+            keep = pltpu.make_async_copy(sent.at[f, rows], last.at[:, me, :], out_sems.at[0])
+            keep.start()
 
     small[2].wait()
     small[5].wait()
@@ -364,48 +372,66 @@
         pltpu.make_async_copy(got.at[f, pl.ds(0, 2016)], got.at[f, pl.ds(0, 2016)], a_send.at[f]).wait()
     pltpu.make_async_copy(taps.at[0, pl.ds(0, 124)], taps.at[0, pl.ds(0, 124)], tap_send).wait()
 
-    for f in range(2):
-        pltpu.make_async_copy(got.at[f, pl.ds(0, 2016)], got.at[f, pl.ds(0, 2016)], b_recv.at[f]).wait()
-
-        def from_planes(i, _):
-            pair = jnp.concatenate([back[f, 2 * i], back[f, 2 * i + 1]], axis=1)
-            h, l = halves(pair)
-            out = jnp.dot(inv_ref[f], jnp.concatenate([h, l, h], axis=0), preferred_element_type=F32)
-            local[2 * i] += out[:, :LANES]
-            local[2 * i + 1] += out[:, LANES:]
+    pltpu.make_async_copy(got.at[0, pl.ds(0, 2016)], got.at[0, pl.ds(0, 2016)], b_recv.at[0]).wait()
+    add_planes(inv_ref, first, local, local)
+    put = pltpu.make_async_copy(local, local_hbm, out_sems.at[1])
+    put.start()
+    for f in range(2):
+        pltpu.make_async_copy(got.at[f, pl.ds(0, 2016)], got.at[f, pl.ds(0, 2016)], b_send.at[f]).wait()
+    keep.wait()
+    put.wait()
+    pltpu.make_async_copy(got.at[1, pl.ds(0, 2016)], got.at[1, pl.ds(0, 2016)], b_recv.at[1]).wait()
+
+
+def finish(local_hbm, last_hbm, inv_hbm, out_hbm, local, last, inv_ref, total, local_sems, last_sems, inv_sem, out_sem):
+    table = pltpu.make_async_copy(inv_hbm, inv_ref, inv_sem)
+    table.start()
+    loads = []
+    for i in range(PARTS):
+        rows = pl.ds(i * 32 // PARTS, 32 // PARTS)
+        loads.append(
+            [
+                pltpu.make_async_copy(last_hbm.at[rows], last.at[rows], last_sems.at[i]),
+                pltpu.make_async_copy(local_hbm.at[rows], local.at[rows], local_sems.at[i]),
+            ]
+        )
+        for copy in loads[i]:
+            copy.start()
+    table.wait()
+    for i in range(PARTS):
+        rows = pl.ds(i * 32 // PARTS, 32 // PARTS)
+        for copy in loads[i]:
+            copy.wait()
+        add_planes(inv_ref, last.at[rows], local.at[rows], total.at[rows])
+
+        def store(p, _):
+            pltpu.make_async_copy(
+                total.at[rows, p, :], out_hbm.at[rows, pl.ds(pl.multiple_of(p * LANES, LANES), LANES)], out_sem
+            ).start()
             return 0
 
-        lax.fori_loop(0, 16, from_planes, 0, unroll=2)
-
-    def store(p, _):
-        pltpu.make_async_copy(
-            local.at[:, p, :], out_hbm.at[:, pl.ds(pl.multiple_of(p * LANES, LANES), LANES)], out_sem
-        ).start()
-        return 0
-
-    lax.fori_loop(0, LANES, store, 0, unroll=8)
-    for f in range(2):
-        pltpu.make_async_copy(got.at[f, pl.ds(0, 2016)], got.at[f, pl.ds(0, 2016)], b_send.at[f]).wait()
-    pltpu.make_async_copy(local, local, out_sem).wait()
+        lax.fori_loop(0, LANES, store, 0, unroll=16)
+    pltpu.make_async_copy(total, total, out_sem).wait()
 
 
 def body(pixels, row_taps, column_taps, stencil):
     fwd, inv = plane_tables()
     hbm = pl.BlockSpec(memory_space=pltpu.HBM)
     block = (32, LANES, LANES)
+    half = (32, PEERS, LANES)
     columns = (2, 2048, LANES)
     dma = pltpu.SemaphoreType.DMA
-    return pl.pallas_call(
+    local, last = pl.pallas_call(
         kernel,
-        out_shape=jax.ShapeDtypeStruct(pixels.shape, F32),
+        out_shape=(jax.ShapeDtypeStruct(block, F32), jax.ShapeDtypeStruct(half, F32)),
         in_specs=[hbm] * 7,
-        out_specs=hbm,
+        out_specs=(hbm, hbm),
         scratch_shapes=[
             pltpu.VMEM((256,), F32),
             pltpu.VMEM((32,), F32),
             pltpu.SMEM((3, 3), F32),
             pltpu.VMEM((256, 256), BF16),
-            pltpu.VMEM((2, LANES, 192), BF16),
+            pltpu.VMEM((LANES, 192), BF16),
             pltpu.VMEM((8, 2 * LANES), F32),
             pltpu.VMEM((4, LANES), F32),
             pltpu.VMEM((2, LANES, LANES), F32),
@@ -415,7 +441,7 @@
             pltpu.VMEM(columns, F32),
             pltpu.VMEM(columns, F32),
             pltpu.VMEM(columns, F32),
-            pltpu.VMEM((2, 32, PEERS, LANES), F32),
+            pltpu.VMEM(half, F32),
             pltpu.VMEM(block, F32),
             pltpu.VMEM((BLOCKS, LANES), F32),
             pltpu.VMEM((BLOCKS, LANES, LANES), F32),
@@ -423,14 +449,29 @@
             pltpu.VMEM((8, 256, 256), BF16),
             pltpu.VMEM((8, 256, LANES), F32),
             pltpu.VMEM((2, 256, 256), BF16),
-            dma, dma, dma((6,)), dma, dma, dma, dma, dma((2,)), dma((2,)),
+            dma, dma((2,)), dma((6,)), dma, dma, dma, dma, dma((2,)), dma((2,)),
             dma((2,)), dma((2,)), dma((2,)), dma((2,)), dma((2,)), dma((2,)),
         ],
         compiler_params=pltpu.CompilerParams(
-            collective_id=0, has_side_effects=True, vmem_limit_bytes=67_043_328
+            collective_id=0, has_side_effects=True, vmem_limit_bytes=MAIN_LIMIT
         ),
         name="filter_rows_and_columns",
-    )(pixels, row_taps, column_taps, stencil, jnp.asarray(tap_tables()), jnp.asarray(fwd), jnp.asarray(inv))
+    )(pixels, row_taps, column_taps, stencil, jnp.asarray(tap_tables()), jnp.asarray(fwd), jnp.asarray(inv[0]))
+    return pl.pallas_call(
+        finish,
+        out_shape=jax.ShapeDtypeStruct(pixels.shape, F32),
+        in_specs=[hbm] * 3,
+        out_specs=hbm,
+        scratch_shapes=[
+            pltpu.VMEM(block, F32),
+            pltpu.VMEM(half, F32),
+            pltpu.VMEM((LANES, 192), BF16),
+            pltpu.VMEM(block, F32),
+            dma((PARTS,)), dma((PARTS,)), dma, dma,
+        ],
+        compiler_params=pltpu.CompilerParams(vmem_limit_bytes=FINISH_LIMIT),
+        name="last_planes",
+    )(local, last, jnp.asarray(inv[1]))
 
 
 def solution(mesh):

time: 66.5 us -> 63.5 us (0.955)
  local copies, waits for them, and re-layouts: 3.05 us -> 0 us
    unnamed x1 -> x0, local copies, waits for them, and re-layouts: 3.05 us -> none
    pallas_call x1 -> x2, Pallas kernels: 63.3 us -> 63.4 us  [the longest x1 59.2 us: body(): pl.pallas_call(kernel, out_shape=(jax.ShapeDtypeStruct(block, F32), jax.S...]
where the time goes in v3:
time: 63.5 us; the launch traced here: 63.4 us
  Pallas kernels  63.4 us (100%)
    pallas_call x1, Pallas kernels, body(): pl.pallas_call(kernel, out_shape=(jax.ShapeDtypeStruct(block, F32), jax.S...  59.2 us
    pallas_call x1, Pallas kernels, body(): pl.pallas_call(finish, out_shape=jax.ShapeDtypeStruct(pixels.shape, F32),...  4.17 us

profile of v3, /device:TPU:1, one launch (start us, length us, event | category | flops | bytes accessed | tf_op | source)
XLA Modules:
  0.0 63.4 jit_solution(8282886768164658634)
XLA Ops:
  0.0 59.2 %filter_rows_and_columns.1 = (f32[32,128,128]{2,1,0:T(8,128)}, f32[32,64,128]{2,1,0:T(8,128)}) custom-call(f32[32,16384]{1,0:T(8,128)} %x_hbm.1, f32[256]{0:T(256)} %row_taps_hbm.1, f32[32]{0:T(128)} %col_taps_hbm.1, f32[3,3]{1,0:T(4,128)} %stencil_hbm.1, f32[64,8,256]{2,1,0:T(8,128)} %constant.8.clone.tab_hbm, bf16[256,256]{1,0:T(8,128)(2,1)} %constant.9.clone.fwd_hbm, ...), custom_call_target="tpu_custom_call" | custom-call | tf_op jit(solution)/shard_map/filter_rows_and_columns/pallas_call | solution.py:424
  59.2 4.2 %last_planes.1 = f32[32,16384]{1,0:T(8,128)} custom-call(f32[32,128,128]{2,1,0:T(8,128)} %get-tuple-element.7.local_hbm, f32[32,64,128]{2,1,0:T(8,128)} %get-tuple-element.8.last_hbm, bf16[128,192]{1,0:T(8,128)(2,1)} %constant.11.clone.inv_hbm), custom_call_target="tpu_custom_call" | custom-call | tf_op jit(solution)/shard_map/last_planes/pallas_call | solution.py:460

commit v4 on v3

--- a/solution.py
+++ b/solution.py
@@ -14,8 +14,8 @@
 PEERS = 64
 LANES = 128
 BLOCKS = 16
-MAIN_LIMIT = 67_043_328
-FINISH_LIMIT = 67_043_328
+MAIN_LIMIT = 48 * 2**20
+FINISH_LIMIT = 32 * 2**20
 PARTS = 1
 GROUP = 7
 
@@ -140,10 +140,10 @@
 
 
 def kernel(
-    x_hbm, row_taps_hbm, col_taps_hbm, stencil_hbm, tab_hbm, fwd_hbm, inv_hbm, local_hbm, last,
+    x_hbm, row_taps_hbm, col_taps_hbm, stencil_hbm, tab_hbm, fwd_hbm, inv_hbm, local, last,
     row_taps, col_taps, stencil, fwd_ref, inv_ref, tab, my_taps, taps,
-    xs, planes, got, done, other, sent, first, local, lines, blocks, left, spec, prod, right,
-    in_sem, out_sems, small_sems, tap_send, tap_recv, share_send, share_recv, halo_send, halo_recv,
+    xs, planes, got, done, other, sent, first, lines, blocks, left, spec, prod, right,
+    in_sems, small_sems, tap_send, tap_recv, share_send, share_recv, halo_send, halo_recv,
     a_send, a_recv, swap_send, swap_recv, b_send, b_recv,
 ):
     me = lax.axis_index("rows")
@@ -151,13 +151,8 @@
     back = (first, last)
     sibling = chip * 2 + 1 - core
 
-    def load(p, _):
-        pltpu.make_async_copy(
-            x_hbm.at[:, pl.ds(pl.multiple_of(p * LANES, LANES), LANES)], xs.at[pl.ds(1, 32), p, :], in_sem
-        ).start()
-        return 0
-
-    lax.fori_loop(0, LANES, load, 0, unroll=8)
+    for y in range(32):
+        pltpu.make_async_copy(x_hbm.at[y // 8, :, y % 8, :], xs.at[1 + y], in_sems.at[y // 8]).start()
     pairs = (
         (row_taps_hbm, row_taps), (col_taps_hbm, col_taps), (stencil_hbm, stencil), (fwd_hbm, fwd_ref),
         (tab_hbm.at[me], tab), (inv_hbm, inv_ref),
@@ -188,7 +183,6 @@
     taps[core, my_tap_rows, :] = my_taps[...]
 
     small[3].wait()
-    pltpu.make_async_copy(xs.at[pl.ds(1, 32)], xs.at[pl.ds(1, 32)], in_sem).wait()
 
     def to_planes(i, _):
         pair = jnp.concatenate([xs[2 * i + 1], xs[2 * i + 2]], axis=1)
@@ -199,7 +193,10 @@
                 planes[f, 2 * i + r] = out[f * PEERS : (f + 1) * PEERS, r * LANES : (r + 1) * LANES]
         return 0
 
-    lax.fori_loop(0, 16, to_planes, 0, unroll=4)
+    for part in range(4):
+        rows = xs.at[pl.ds(1 + 8 * part, 8)]
+        pltpu.make_async_copy(rows, rows, in_sems.at[part]).wait()
+        lax.fori_loop(4 * part, 4 * part + 4, to_planes, 0, unroll=4)
     pl.semaphore_wait(barrier, PEERS - 1)
 
     def remote(src, dst, send, recv, to):
@@ -331,23 +328,22 @@
             out = jnp.dot(h, right[f], preferred_element_type=F32)
             return out[:, :LANES] + out[:, LANES:] + jnp.dot(l, right[f, :, 0:LANES], preferred_element_type=F32)
 
-        for j in range(0, PEERS - 1, GROUP):
-            owners = peers[j : j + GROUP]
+        def send_back(owners):
+            for to in owners:
+                rows = pl.ds(pl.multiple_of(to * 32, 32), 32)
+                remote(sent.at[f, rows], back[f].at[:, me, :], b_send.at[f], b_recv.at[f], to).start()
+
+        groups = [peers[j : j + GROUP] for j in range(0, PEERS - 1, GROUP)]
+        for j, owners in enumerate(groups):
             out = product(owners)
             for k, to in enumerate(owners):
-                rows = pl.ds(pl.multiple_of(to * 32, 32), 32)
-                sent[f, rows, :] = out[k * 32 : (k + 1) * 32]
-                remote(sent.at[f, rows], back[f].at[:, me, :], b_send.at[f], b_recv.at[f], to).start()
-
+                sent[f, pl.ds(pl.multiple_of(to * 32, 32), 32), :] = out[k * 32 : (k + 1) * 32]
+            if j:
+                send_back(groups[j - 1])
+        send_back(groups[-1])
         mine = product([me])
-        if f == 0:
-            for r in range(32):
-                first[r, pl.ds(me, 1), :] = mine[r : r + 1]
-        else:
-            rows = pl.ds(pl.multiple_of(me * 32, 32), 32)
-            sent[f, rows, :] = mine
-            keep = pltpu.make_async_copy(sent.at[f, rows], last.at[:, me, :], out_sems.at[0])
-            keep.start()
+        for r in range(32):
+            back[f][r, pl.ds(me, 1), :] = mine[r : r + 1]
 
     small[2].wait()
     small[5].wait()
@@ -374,58 +370,43 @@
 
     pltpu.make_async_copy(got.at[0, pl.ds(0, 2016)], got.at[0, pl.ds(0, 2016)], b_recv.at[0]).wait()
     add_planes(inv_ref, first, local, local)
-    put = pltpu.make_async_copy(local, local_hbm, out_sems.at[1])
-    put.start()
     for f in range(2):
         pltpu.make_async_copy(got.at[f, pl.ds(0, 2016)], got.at[f, pl.ds(0, 2016)], b_send.at[f]).wait()
-    keep.wait()
-    put.wait()
     pltpu.make_async_copy(got.at[1, pl.ds(0, 2016)], got.at[1, pl.ds(0, 2016)], b_recv.at[1]).wait()
 
 
-def finish(local_hbm, last_hbm, inv_hbm, out_hbm, local, last, inv_ref, total, local_sems, last_sems, inv_sem, out_sem):
-    table = pltpu.make_async_copy(inv_hbm, inv_ref, inv_sem)
-    table.start()
-    loads = []
-    for i in range(PARTS):
-        rows = pl.ds(i * 32 // PARTS, 32 // PARTS)
-        loads.append(
-            [
-                pltpu.make_async_copy(last_hbm.at[rows], last.at[rows], last_sems.at[i]),
-                pltpu.make_async_copy(local_hbm.at[rows], local.at[rows], local_sems.at[i]),
-            ]
-        )
-        for copy in loads[i]:
-            copy.start()
-    table.wait()
-    for i in range(PARTS):
-        rows = pl.ds(i * 32 // PARTS, 32 // PARTS)
-        for copy in loads[i]:
-            copy.wait()
+def finish(local, last, inv_ref, out_hbm, total, out_sem):
+    def store(y):
+        pltpu.make_async_copy(total.at[y], out_hbm.at[y // 8, :, y % 8, :], out_sem).start()
+
+    for part in range(PARTS):
+        rows = pl.ds(part * 32 // PARTS, 32 // PARTS)
         add_planes(inv_ref, last.at[rows], local.at[rows], total.at[rows])
-
-        def store(p, _):
-            pltpu.make_async_copy(
-                total.at[rows, p, :], out_hbm.at[rows, pl.ds(pl.multiple_of(p * LANES, LANES), LANES)], out_sem
-            ).start()
-            return 0
-
-        lax.fori_loop(0, LANES, store, 0, unroll=16)
+        for y in range(part * 32 // PARTS, (part + 1) * 32 // PARTS):
+            store(y)
     pltpu.make_async_copy(total, total, out_sem).wait()
+
+
+def tiles(image):
+    return image.reshape(4, 8, LANES, LANES).transpose(0, 2, 1, 3)
 
 
 def body(pixels, row_taps, column_taps, stencil):
     fwd, inv = plane_tables()
-    hbm = pl.BlockSpec(memory_space=pltpu.HBM)
+    hbm, vmem = pl.BlockSpec(memory_space=pltpu.HBM), pl.BlockSpec(memory_space=pltpu.VMEM)
     block = (32, LANES, LANES)
     half = (32, PEERS, LANES)
     columns = (2, 2048, LANES)
     dma = pltpu.SemaphoreType.DMA
+    operands = (
+        tiles(pixels), row_taps, column_taps, stencil,
+        jnp.asarray(tap_tables()), jnp.asarray(fwd), jnp.asarray(inv[0]),
+    )
     local, last = pl.pallas_call(
         kernel,
-        out_shape=(jax.ShapeDtypeStruct(block, F32), jax.ShapeDtypeStruct(half, F32)),
+        out_shape=(pltpu.VMEM(block, F32), pltpu.VMEM(half, F32)),
         in_specs=[hbm] * 7,
-        out_specs=(hbm, hbm),
+        out_specs=(vmem, vmem),
         scratch_shapes=[
             pltpu.VMEM((256,), F32),
             pltpu.VMEM((32,), F32),
@@ -442,36 +423,30 @@
             pltpu.VMEM(columns, F32),
             pltpu.VMEM(columns, F32),
             pltpu.VMEM(half, F32),
-            pltpu.VMEM(block, F32),
             pltpu.VMEM((BLOCKS, LANES), F32),
             pltpu.VMEM((BLOCKS, LANES, LANES), F32),
             pltpu.VMEM((8, 512, 256), BF16),
             pltpu.VMEM((8, 256, 256), BF16),
             pltpu.VMEM((8, 256, LANES), F32),
             pltpu.VMEM((2, 256, 256), BF16),
-            dma, dma((2,)), dma((6,)), dma, dma, dma, dma, dma((2,)), dma((2,)),
+            dma((4,)), dma((6,)), dma, dma, dma, dma, dma((2,)), dma((2,)),
             dma((2,)), dma((2,)), dma((2,)), dma((2,)), dma((2,)), dma((2,)),
         ],
         compiler_params=pltpu.CompilerParams(
             collective_id=0, has_side_effects=True, vmem_limit_bytes=MAIN_LIMIT
         ),
         name="filter_rows_and_columns",
-    )(pixels, row_taps, column_taps, stencil, jnp.asarray(tap_tables()), jnp.asarray(fwd), jnp.asarray(inv[0]))
-    return pl.pallas_call(
+    )(*(pltpu.with_memory_space_constraint(operand, pltpu.HBM) for operand in operands))
+    out = pl.pallas_call(
         finish,
-        out_shape=jax.ShapeDtypeStruct(pixels.shape, F32),
-        in_specs=[hbm] * 3,
+        out_shape=jax.ShapeDtypeStruct((4, LANES, 8, LANES), F32),
+        in_specs=[vmem] * 3,
         out_specs=hbm,
-        scratch_shapes=[
-            pltpu.VMEM(block, F32),
-            pltpu.VMEM(half, F32),
-            pltpu.VMEM((LANES, 192), BF16),
-            pltpu.VMEM(block, F32),
-            dma((PARTS,)), dma((PARTS,)), dma, dma,
-        ],
+        scratch_shapes=[pltpu.VMEM(block, F32), dma],
         compiler_params=pltpu.CompilerParams(vmem_limit_bytes=FINISH_LIMIT),
         name="last_planes",
     )(local, last, jnp.asarray(inv[1]))
+    return out.transpose(0, 2, 1, 3).reshape(pixels.shape)
 
 
 def solution(mesh):

time: 63.5 us -> 61.7 us (0.972)
  Pallas kernels: 63.4 us -> 61.5 us
    pallas_call x2, Pallas kernels: 63.4 us -> 61.5 us  [the longest x1 59.3 us: body(): pl.pallas_call(kernel, out_shape=(pltpu.VMEM(block, F32), pltpu.VMEM(half...]
where the time goes in v4:
time: 61.7 us; the launch traced here: 61.5 us
  Pallas kernels  61.5 us (100%)
    pallas_call x1, Pallas kernels, body(): pl.pallas_call(kernel, out_shape=(pltpu.VMEM(block, F32), pltpu.VMEM(half...  59.3 us
    pallas_call x1, Pallas kernels, body(): pl.pallas_call(finish, out_shape=jax.ShapeDtypeStruct((4, LANES, 8, LANES...  2.2 us

profile of v4, /device:TPU:1, one launch (start us, length us, event | category | flops | bytes accessed | tf_op | source)
XLA Modules:
  0.0 61.5 jit_solution(8710896614669371822)
XLA Ops:
  0.0 0.0 copy-start
  0.0 59.3 %filter_rows_and_columns.1 = (f32[32,128,128]{2,1,0:T(8,128)S(1)}, f32[32,64,128]{2,1,0:T(8,128)S(1)}) custom-call(f32[4,128,8,128]{3,2,1,0:T(8,128)} %bitcast.6, f32[256]{0:T(256)} %row_taps_hbm.1, f32[32]{0:T(128)} %col_taps_hbm.1, f32[3,3]{1,0:T(4,128)} %stencil_hbm.1, f32[64,8,256]{2,1,0:T(8,128)} %constant.8.clone.tab_hbm, ...), custom_call_target="tpu_custom_call" | custom-call | tf_op jit(solution)/shard_map/filter_rows_and_columns/pallas_call | solution.py:405
  59.3 0.0 copy-done
  59.3 2.2 %last_planes.1 = f32[4,128,8,128]{3,2,1,0:T(8,128)} custom-call(f32[32,128,128]{2,1,0:T(8,128)S(1)} %get-tuple-element.7.local, f32[32,64,128]{2,1,0:T(8,128)S(1)} %get-tuple-element.8.last, bf16[128,192]{1,0:T(8,128)(2,1)S(1)} %copy-done), custom_call_target="tpu_custom_call" | custom-call | tf_op jit(solution)/shard_map/last_planes/pallas_call | solution.py:440
Async XLA Ops:
  0.0 59.3 %copy-start = (bf16[128,192]{1,0:T(8,128)(2,1)S(1)}, bf16[128,192]{1,0:T(8,128)(2,1)}, u32[]{:S(2)}) copy-start(bf16[128,192]{1,0:T(8,128)(2,1)} %constant.11.clone.inv_ref) | copy-start | bytes 147460

commit v5 on v4

--- a/solution.py
+++ b/solution.py
@@ -16,11 +16,16 @@
 BLOCKS = 16
 MAIN_LIMIT = 48 * 2**20
 FINISH_LIMIT = 32 * 2**20
-PARTS = 1
+PARTS = 4
 GROUP = 7
 
 
-STEPS = [(i * (i + 1) // 2) % PEERS for i in range(1, PEERS)]
+STEPS = [
+    52, 1, 53, 33, 21, 3, 55, 8, 61, 32, 20, 6, 50, 9, 60, 2,
+    54, 25, 44, 7, 51, 24, 45, 35, 23, 30, 43, 27, 47, 5, 49, 11,
+    63, 34, 22, 15, 58, 41, 28, 16, 36, 31, 42, 17, 37, 56, 12, 14,
+    59, 26, 46, 38, 19, 57, 13, 39, 18, 10, 62, 40, 29, 4, 48,
+]
 
 
 def split_np(values):
@@ -143,7 +148,7 @@
     x_hbm, row_taps_hbm, col_taps_hbm, stencil_hbm, tab_hbm, fwd_hbm, inv_hbm, local, last,
     row_taps, col_taps, stencil, fwd_ref, inv_ref, tab, my_taps, taps,
     xs, planes, got, done, other, sent, first, lines, blocks, left, spec, prod, right,
-    in_sems, small_sems, tap_send, tap_recv, share_send, share_recv, halo_send, halo_recv,
+    in_sem, small_sems, tap_send, tap_recv, share_send, share_recv, halo_send, halo_recv,
     a_send, a_recv, swap_send, swap_recv, b_send, b_recv,
 ):
     me = lax.axis_index("rows")
@@ -152,7 +157,7 @@
     sibling = chip * 2 + 1 - core
 
     for y in range(32):
-        pltpu.make_async_copy(x_hbm.at[y // 8, :, y % 8, :], xs.at[1 + y], in_sems.at[y // 8]).start()
+        pltpu.make_async_copy(x_hbm.at[y // 8, :, y % 8, :], xs.at[1 + y], in_sem).start()
     pairs = (
         (row_taps_hbm, row_taps), (col_taps_hbm, col_taps), (stencil_hbm, stencil), (fwd_hbm, fwd_ref),
         (tab_hbm.at[me], tab), (inv_hbm, inv_ref),
@@ -193,10 +198,9 @@
                 planes[f, 2 * i + r] = out[f * PEERS : (f + 1) * PEERS, r * LANES : (r + 1) * LANES]
         return 0
 
-    for part in range(4):
-        rows = xs.at[pl.ds(1 + 8 * part, 8)]
-        pltpu.make_async_copy(rows, rows, in_sems.at[part]).wait()
-        lax.fori_loop(4 * part, 4 * part + 4, to_planes, 0, unroll=4)
+    rows = xs.at[pl.ds(1, 32)]
+    pltpu.make_async_copy(rows, rows, in_sem).wait()
+    lax.fori_loop(0, 16, to_planes, 0, unroll=16)
     pl.semaphore_wait(barrier, PEERS - 1)
 
     def remote(src, dst, send, recv, to):
@@ -292,7 +296,7 @@
                     spec[k, rows, LANES : 2 * LANES] = l
             return 0
 
-        lax.fori_loop(0, 8, spectrum, 0)
+        lax.fori_loop(0, 8, spectrum, 0, unroll=2)
 
         def multiply(k, _):
             out = jnp.dot(left[k], spec[k], preferred_element_type=F32)
@@ -300,7 +304,7 @@
             prod[k] = out[:, :LANES] + out[:, LANES:]
             return 0
 
-        lax.fori_loop(0, 8, multiply, 0)
+        lax.fori_loop(0, 8, multiply, 0, unroll=2)
 
         def unspectrum(t, _):
             freqs = []
@@ -314,7 +318,7 @@
                 done[f, pl.ds(pl.multiple_of(b * LANES + t * 16, 16), 16), :] = value
             return 0
 
-        lax.fori_loop(0, 8, unspectrum, 0)
+        lax.fori_loop(0, 8, unspectrum, 0, unroll=2)
         swap = remote(done.at[f], other.at[f], swap_send.at[f], swap_recv.at[f], sibling)
         swap.start()
         swap.wait()
@@ -429,7 +433,7 @@
             pltpu.VMEM((8, 256, 256), BF16),
             pltpu.VMEM((8, 256, LANES), F32),
             pltpu.VMEM((2, 256, 256), BF16),
-            dma((4,)), dma((6,)), dma, dma, dma, dma, dma((2,)), dma((2,)),
+            dma, dma((6,)), dma, dma, dma, dma, dma((2,)), dma((2,)),
             dma((2,)), dma((2,)), dma((2,)), dma((2,)), dma((2,)), dma((2,)),
         ],
         compiler_params=pltpu.CompilerParams(

time: 61.7 us -> 59.4 us (0.963)
  Pallas kernels: 61.5 us -> 59.3 us
    pallas_call x1, Pallas kernels: 59.3 us -> 57.7 us  [body(): pl.pallas_call(kernel, out_shape=(pltpu.VMEM(block, F32), pltpu.VMEM(half...]
    pallas_call x1, Pallas kernels: 2.2 us -> 1.52 us  [body(): pl.pallas_call(finish, out_shape=jax.ShapeDtypeStruct((4, LANES, 8, LANES...]
where the time goes in v5:
time: 59.4 us; the launch traced here: 59.3 us
  Pallas kernels  59.3 us (100%)
    pallas_call x1, Pallas kernels, body(): pl.pallas_call(kernel, out_shape=(pltpu.VMEM(block, F32), pltpu.VMEM(half...  57.7 us
    pallas_call x1, Pallas kernels, body(): pl.pallas_call(finish, out_shape=jax.ShapeDtypeStruct((4, LANES, 8, LANES...  1.52 us

profile of v5, /device:TPU:1, one launch (start us, length us, event | category | flops | bytes accessed | tf_op | source)
XLA Modules:
  0.0 59.3 jit_solution(2267898602931717210)
XLA Ops:
  0.0 0.0 copy-start
  0.0 57.7 %filter_rows_and_columns.1 = (f32[32,128,128]{2,1,0:T(8,128)S(1)}, f32[32,64,128]{2,1,0:T(8,128)S(1)}) custom-call(f32[4,128,8,128]{3,2,1,0:T(8,128)} %bitcast.6, f32[256]{0:T(256)} %row_taps_hbm.1, f32[32]{0:T(128)} %col_taps_hbm.1, f32[3,3]{1,0:T(4,128)} %stencil_hbm.1, f32[64,8,256]{2,1,0:T(8,128)} %constant.8.clone.tab_hbm, ...), custom_call_target="tpu_custom_call" | custom-call | tf_op jit(solution)/shard_map/filter_rows_and_columns/pallas_call | solution.py:409
  57.8 0.0 copy-done
  57.8 1.5 %last_planes.1 = f32[4,128,8,128]{3,2,1,0:T(8,128)} custom-call(f32[32,128,128]{2,1,0:T(8,128)S(1)} %get-tuple-element.7.local, f32[32,64,128]{2,1,0:T(8,128)S(1)} %get-tuple-element.8.last, bf16[128,192]{1,0:T(8,128)(2,1)S(1)} %copy-done), custom_call_target="tpu_custom_call" | custom-call | tf_op jit(solution)/shard_map/last_planes/pallas_call | solution.py:444
Async XLA Ops:
  0.0 57.8 %copy-start = (bf16[128,192]{1,0:T(8,128)(2,1)S(1)}, bf16[128,192]{1,0:T(8,128)(2,1)}, u32[]{:S(2)}) copy-start(bf16[128,192]{1,0:T(8,128)(2,1)} %constant.11.clone.inv_ref) | copy-start | bytes 147460

commit v6 on v5

--- a/solution.py
+++ b/solution.py
@@ -17,6 +17,7 @@
 MAIN_LIMIT = 48 * 2**20
 FINISH_LIMIT = 32 * 2**20
 PARTS = 4
+EDGE = 8
 GROUP = 7
 
 
@@ -137,8 +138,9 @@
     def step(i, _):
         h, l = halves(jnp.concatenate([planes[2 * i], planes[2 * i + 1]], axis=1))
         out = jnp.dot(table_ref[...], jnp.concatenate([h, l, h], axis=0), preferred_element_type=F32)
-        total[2 * i] = base[2 * i] + out[:, :LANES]
-        total[2 * i + 1] = base[2 * i + 1] + out[:, LANES:]
+        for r in range(2):
+            part = out[:, r * LANES : (r + 1) * LANES]
+            total[2 * i + r] = part if base is None else base[2 * i + r] + part
         return 0
 
     lax.fori_loop(0, total.shape[0] // 2, step, 0, unroll=4)
@@ -147,8 +149,8 @@
 def kernel(
     x_hbm, row_taps_hbm, col_taps_hbm, stencil_hbm, tab_hbm, fwd_hbm, inv_hbm, local, last,
     row_taps, col_taps, stencil, fwd_ref, inv_ref, tab, my_taps, taps,
-    xs, planes, got, done, other, sent, first, lines, blocks, left, spec, prod, right,
-    in_sem, small_sems, tap_send, tap_recv, share_send, share_recv, halo_send, halo_recv,
+    xs, planes, got, raw, done, other, sent, first, lines, blocks, left, spec, prod, right,
+    in_sem, small_sems, tap_send, tap_recv, share_send, share_recv,
     a_send, a_recv, swap_send, swap_recv, b_send, b_recv,
 ):
     me = lax.axis_index("rows")
@@ -157,7 +159,7 @@
     sibling = chip * 2 + 1 - core
 
     for y in range(32):
-        pltpu.make_async_copy(x_hbm.at[y // 8, :, y % 8, :], xs.at[1 + y], in_sem).start()
+        pltpu.make_async_copy(x_hbm.at[y // 8, :, y % 8, :], xs.at[y], in_sem).start()
     pairs = (
         (row_taps_hbm, row_taps), (col_taps_hbm, col_taps), (stencil_hbm, stencil), (fwd_hbm, fwd_ref),
         (tab_hbm.at[me], tab), (inv_hbm, inv_ref),
@@ -190,7 +192,7 @@
     small[3].wait()
 
     def to_planes(i, _):
-        pair = jnp.concatenate([xs[2 * i + 1], xs[2 * i + 2]], axis=1)
+        pair = jnp.concatenate([xs[2 * i], xs[2 * i + 1]], axis=1)
         out = jnp.dot(fwd_ref[...], jnp.concatenate(halves(pair), axis=0), preferred_element_type=F32)
         out = out[:LANES] + out[LANES:]
         for f in range(2):
@@ -198,8 +200,7 @@
                 planes[f, 2 * i + r] = out[f * PEERS : (f + 1) * PEERS, r * LANES : (r + 1) * LANES]
         return 0
 
-    rows = xs.at[pl.ds(1, 32)]
-    pltpu.make_async_copy(rows, rows, in_sem).wait()
+    pltpu.make_async_copy(xs, xs, in_sem).wait()
     lax.fori_loop(0, 16, to_planes, 0, unroll=16)
     pl.semaphore_wait(barrier, PEERS - 1)
 
@@ -215,21 +216,16 @@
         for to in peers:
             remote(
                 planes.at[f, :, to, :],
-                got.at[f, pl.ds(pl.multiple_of(me * 32, 32), 32)],
+                got.at[f, pl.ds(pl.multiple_of(me * 32 + EDGE, EDGE), 32)],
                 a_send.at[f],
                 a_recv.at[f],
                 to,
             ).start()
 
-    down = remote(xs.at[32], xs.at[0], halo_send.at[0], halo_recv.at[0], (me + 1) % PEERS)
-    up = remote(xs.at[1], xs.at[33], halo_send.at[1], halo_recv.at[1], (me + PEERS - 1) % PEERS)
-    down.start()
-    up.start()
-
     for f in range(2):
 
         def own(r, _):
-            got[f, pl.ds(me * 32 + r, 1), :] = planes[f, r, pl.ds(me, 1), :]
+            got[f, pl.ds(me * 32 + EDGE + r, 1), :] = planes[f, r, pl.ds(me, 1), :]
             return 0
 
         lax.fori_loop(0, 32, own, 0)
@@ -242,15 +238,23 @@
     g = jnp.dot(tab[:, 0:LANES], taps[0], preferred_element_type=F32, precision=lax.Precision.HIGHEST)
     g = g + jnp.dot(tab[:, LANES:], taps[1], preferred_element_type=F32, precision=lax.Precision.HIGHEST)
     sign = (2 * core - 1).astype(F32)
-    for f in range(2):
-        gr, gi = g[2 * f : 2 * f + 1], g[2 * f + 1 : 2 * f + 2]
+    small[2].wait()
+    lane = lax.broadcasted_iota(jnp.int32, (1, LANES), 1)
+    for f in range(2):
         wr, wi = tab[4 + 2 * f : 5 + 2 * f, 0:LANES], tab[5 + 2 * f : 6 + 2 * f, 0:LANES]
-        same = toeplitz(jnp.concatenate([gr, wr * gr - wi * gi], axis=1))
-        cross = toeplitz(jnp.concatenate([gi, wr * gi + wi * gr], axis=1) * sign)
-        for r, value in enumerate((same, cross)):
-            h, l = halves(value)
-            right[f, r * LANES : (r + 1) * LANES, 0:LANES] = h
-            right[f, r * LANES : (r + 1) * LANES, LANES : 2 * LANES] = l
+        lines_of = [(g[2 * f : 2 * f + 1], g[2 * f + 1 : 2 * f + 2])]
+        for a in range(3):
+            ahead = jnp.where(lane == LANES - 1, stencil[a, 2], 0.0)
+            here = jnp.where(lane == 0, stencil[a, 1], 0.0) + jnp.where(lane == 1, stencil[a, 0], 0.0)
+            lines_of.append((here + ahead * wr, -ahead * wi))
+        for part, (gr, gi) in enumerate(lines_of):
+            same = toeplitz(jnp.concatenate([gr, wr * gr - wi * gi], axis=1))
+            cross = toeplitz(jnp.concatenate([gi, wr * gi + wi * gr], axis=1) * sign)
+            for r, value in enumerate((same, cross)):
+                h, l = halves(value)
+                at = (2 * part + r) * LANES
+                right[f, at : at + LANES, 0:LANES] = h
+                right[f, at : at + LANES, LANES : 2 * LANES] = l
 
     lines[...] = sum(taps[c, pl.ds(4 * e + 2, BLOCKS, stride=8), :] for e in range(2) for c in range(2))
 
@@ -285,7 +289,7 @@
 
         def spectrum(t, _):
             freqs = rfft(
-                [got[f, pl.ds(pl.multiple_of(b * LANES + t * 16, 16), 16), :] for b in range(BLOCKS)]
+                [got[f, pl.ds(pl.multiple_of(b * LANES + t * 16 + EDGE, EDGE), 16), :] for b in range(BLOCKS)]
             )
             for k in range(8):
                 pair = (freqs[0][0], freqs[8][0]) if k == 0 else freqs[k]
@@ -296,7 +300,11 @@
                     spec[k, rows, LANES : 2 * LANES] = l
             return 0
 
+        got[f, 0:EDGE, :] = got[f, 2048 : 2048 + EDGE, :]
+        got[f, 2048 + EDGE : 2048 + 2 * EDGE, :] = got[f, EDGE : 2 * EDGE, :]
         lax.fori_loop(0, 8, spectrum, 0, unroll=2)
+        share_raw = remote(got.at[f], raw.at[f], swap_send.at[2 + f], swap_recv.at[2 + f], sibling)
+        share_raw.start()
 
         def multiply(k, _):
             out = jnp.dot(left[k], spec[k], preferred_element_type=F32)
@@ -321,14 +329,19 @@
         lax.fori_loop(0, 8, unspectrum, 0, unroll=2)
         swap = remote(done.at[f], other.at[f], swap_send.at[f], swap_recv.at[f], sibling)
         swap.start()
+        share_raw.wait()
         swap.wait()
 
         def product(owners):
             rows = [pl.ds(pl.multiple_of(t * 32, 32), 32) for t in owners]
-            both = [
-                jnp.concatenate([ref[f, r, :] for r in rows], axis=0) for ref in (done, other)
+            parts = [jnp.concatenate([ref[f, r, :] for r in rows], axis=0) for ref in (done, other)]
+            near = [
+                [ref[f, pl.ds(pl.multiple_of(t * 32, 32), 32 + 2 * EDGE), :] for t in owners] for ref in (got, raw)
             ]
-            h, l = halves(jnp.concatenate(both, axis=1))
+            for a in range(3):
+                first_row = EDGE - 1 + a
+                parts += [jnp.concatenate([v[first_row : first_row + 32] for v in vs], axis=0) for vs in near]
+            h, l = halves(jnp.concatenate(parts, axis=1))
             out = jnp.dot(h, right[f], preferred_element_type=F32)
             return out[:, :LANES] + out[:, LANES:] + jnp.dot(l, right[f, :, 0:LANES], preferred_element_type=F32)
 
@@ -349,31 +362,13 @@
         for r in range(32):
             back[f][r, pl.ds(me, 1), :] = mine[r : r + 1]
 
-    small[2].wait()
     small[5].wait()
-    down.wait()
-    up.wait()
-    lane = lax.broadcasted_iota(jnp.int32, (LANES, LANES), 1)
-
-    def stencil_row(y, _):
-        total = jnp.zeros((LANES, LANES), F32)
-        for a in range(3):
-            here = xs[y + a]
-            before, after = pltpu.roll(here, 1, 1), pltpu.roll(here, LANES - 1, 1)
-            before = jnp.where(lane == 0, pltpu.roll(before, 1, 0), before)
-            after = jnp.where(lane == LANES - 1, pltpu.roll(after, LANES - 1, 0), after)
-            total = total + stencil[a, 0] * before + stencil[a, 1] * here + stencil[a, 2] * after
-        local[y] = total
-        return 0
-
-    lax.fori_loop(0, 32, stencil_row, 0)
-
     for f in range(2):
         pltpu.make_async_copy(got.at[f, pl.ds(0, 2016)], got.at[f, pl.ds(0, 2016)], a_send.at[f]).wait()
     pltpu.make_async_copy(taps.at[0, pl.ds(0, 124)], taps.at[0, pl.ds(0, 124)], tap_send).wait()
 
     pltpu.make_async_copy(got.at[0, pl.ds(0, 2016)], got.at[0, pl.ds(0, 2016)], b_recv.at[0]).wait()
-    add_planes(inv_ref, first, local, local)
+    add_planes(inv_ref, first, None, local)
     for f in range(2):
         pltpu.make_async_copy(got.at[f, pl.ds(0, 2016)], got.at[f, pl.ds(0, 2016)], b_send.at[f]).wait()
     pltpu.make_async_copy(got.at[1, pl.ds(0, 2016)], got.at[1, pl.ds(0, 2016)], b_recv.at[1]).wait()
@@ -400,7 +395,7 @@
     hbm, vmem = pl.BlockSpec(memory_space=pltpu.HBM), pl.BlockSpec(memory_space=pltpu.VMEM)
     block = (32, LANES, LANES)
     half = (32, PEERS, LANES)
-    columns = (2, 2048, LANES)
+    columns, edged = (2, 2048, LANES), (2, 2048 + 2 * EDGE, LANES)
     dma = pltpu.SemaphoreType.DMA
     operands = (
         tiles(pixels), row_taps, column_taps, stencil,
@@ -420,9 +415,10 @@
             pltpu.VMEM((8, 2 * LANES), F32),
             pltpu.VMEM((4, LANES), F32),
             pltpu.VMEM((2, LANES, LANES), F32),
-            pltpu.VMEM((34, LANES, LANES), F32),
+            pltpu.VMEM(block, F32),
             pltpu.VMEM((2, 32, PEERS, LANES), F32),
-            pltpu.VMEM(columns, F32),
+            pltpu.VMEM(edged, F32),
+            pltpu.VMEM(edged, F32),
             pltpu.VMEM(columns, F32),
             pltpu.VMEM(columns, F32),
             pltpu.VMEM(columns, F32),
@@ -432,9 +428,9 @@
             pltpu.VMEM((8, 512, 256), BF16),
             pltpu.VMEM((8, 256, 256), BF16),
             pltpu.VMEM((8, 256, LANES), F32),
-            pltpu.VMEM((2, 256, 256), BF16),
-            dma, dma((6,)), dma, dma, dma, dma, dma((2,)), dma((2,)),
-            dma((2,)), dma((2,)), dma((2,)), dma((2,)), dma((2,)), dma((2,)),
+            pltpu.VMEM((2, 1024, 256), BF16),
+            dma, dma((6,)), dma, dma, dma, dma,
+            dma((2,)), dma((2,)), dma((4,)), dma((4,)), dma((2,)), dma((2,)),
         ],
         compiler_params=pltpu.CompilerParams(
             collective_id=0, has_side_effects=True, vmem_limit_bytes=MAIN_LIMIT

time: 59.4 us -> 58.6 us (0.987)
  Pallas kernels: 59.3 us -> 58.5 us
    pallas_call x1, Pallas kernels: 57.7 us -> 56.9 us  [body(): pl.pallas_call(kernel, out_shape=(pltpu.VMEM(block, F32), pltpu.VMEM(half...]
where the time goes in v6:
time: 58.6 us; the launch traced here: 58.5 us
  Pallas kernels  58.5 us (100%)
    pallas_call x1, Pallas kernels, body(): pl.pallas_call(kernel, out_shape=(pltpu.VMEM(block, F32), pltpu.VMEM(half...  56.9 us
    pallas_call x1, Pallas kernels, body(): pl.pallas_call(finish, out_shape=jax.ShapeDtypeStruct((4, LANES, 8, LANES...  1.52 us

profile of v6, /device:TPU:1, one launch (start us, length us, event | category | flops | bytes accessed | tf_op | source)
XLA Modules:
  0.0 58.5 jit_solution(11414133040939695033)
XLA Ops:
  0.0 0.0 copy-start
  0.0 56.9 %filter_rows_and_columns.1 = (f32[32,128,128]{2,1,0:T(8,128)S(1)}, f32[32,64,128]{2,1,0:T(8,128)S(1)}) custom-call(f32[4,128,8,128]{3,2,1,0:T(8,128)} %bitcast.6, f32[256]{0:T(256)} %row_taps_hbm.1, f32[32]{0:T(128)} %col_taps_hbm.1, f32[3,3]{1,0:T(4,128)} %stencil_hbm.1, f32[64,8,256]{2,1,0:T(8,128)} %constant.8.clone.tab_hbm, ...), custom_call_target="tpu_custom_call" | custom-call | tf_op jit(solution)/shard_map/filter_rows_and_columns/pallas_call | solution.py:404
  57.0 0.0 copy-done
  57.0 1.5 %last_planes.1 = f32[4,128,8,128]{3,2,1,0:T(8,128)} custom-call(f32[32,128,128]{2,1,0:T(8,128)S(1)} %get-tuple-element.7.local, f32[32,64,128]{2,1,0:T(8,128)S(1)} %get-tuple-element.8.last, bf16[128,192]{1,0:T(8,128)(2,1)S(1)} %copy-done), custom_call_target="tpu_custom_call" | custom-call | tf_op jit(solution)/shard_map/last_planes/pallas_call | solution.py:440
Async XLA Ops:
  0.0 57.0 %copy-start = (bf16[128,192]{1,0:T(8,128)(2,1)S(1)}, bf16[128,192]{1,0:T(8,128)(2,1)}, u32[]{:S(2)}) copy-start(bf16[128,192]{1,0:T(8,128)(2,1)} %constant.11.clone.inv_ref) | copy-start | bytes 147460

commit v7 on v6

--- a/solution.py
+++ b/solution.py
@@ -22,10 +22,10 @@
 
 
 STEPS = [
-    52, 1, 53, 33, 21, 3, 55, 8, 61, 32, 20, 6, 50, 9, 60, 2,
-    54, 25, 44, 7, 51, 24, 45, 35, 23, 30, 43, 27, 47, 5, 49, 11,
-    63, 34, 22, 15, 58, 41, 28, 16, 36, 31, 42, 17, 37, 56, 12, 14,
-    59, 26, 46, 38, 19, 57, 13, 39, 18, 10, 62, 40, 29, 4, 48,
+    52, 1, 53, 24, 44, 7, 51, 25, 45, 3, 54, 32, 20, 33, 21, 6,
+    50, 2, 55, 8, 61, 9, 60, 34, 22, 38, 18, 56, 12, 11, 63, 35,
+    23, 4, 49, 26, 46, 30, 42, 5, 48, 27, 47, 41, 29, 57, 13, 14,
+    59, 16, 37, 31, 43, 40, 28, 10, 62, 17, 36, 39, 19, 15, 58,
 ]
 
 

time: 58.6 us -> 58.7 us (level)
  no operation moved by 1% of the time
where the time goes in v7:
time: 58.7 us; the launch traced here: 58.5 us
  Pallas kernels  58.5 us (100%)
    pallas_call x1, Pallas kernels, body(): pl.pallas_call(kernel, out_shape=(pltpu.VMEM(block, F32), pltpu.VMEM(half...  57 us
    pallas_call x1, Pallas kernels, body(): pl.pallas_call(finish, out_shape=jax.ShapeDtypeStruct((4, LANES, 8, LANES...  1.52 us

profile of v7, /device:TPU:1, one launch (start us, length us, event | category | flops | bytes accessed | tf_op | source)
XLA Modules:
  0.0 58.5 jit_solution(1015595799777703935)
XLA Ops:
  0.0 0.0 copy-start
  0.0 57.0 %filter_rows_and_columns.1 = (f32[32,128,128]{2,1,0:T(8,128)S(1)}, f32[32,64,128]{2,1,0:T(8,128)S(1)}) custom-call(f32[4,128,8,128]{3,2,1,0:T(8,128)} %bitcast.6, f32[256]{0:T(256)} %row_taps_hbm.1, f32[32]{0:T(128)} %col_taps_hbm.1, f32[3,3]{1,0:T(4,128)} %stencil_hbm.1, f32[64,8,256]{2,1,0:T(8,128)} %constant.8.clone.tab_hbm, ...), custom_call_target="tpu_custom_call" | custom-call | tf_op jit(solution)/shard_map/filter_rows_and_columns/pallas_call | solution.py:404
  57.0 0.0 copy-done
  57.0 1.5 %last_planes.1 = f32[4,128,8,128]{3,2,1,0:T(8,128)} custom-call(f32[32,128,128]{2,1,0:T(8,128)S(1)} %get-tuple-element.7.local, f32[32,64,128]{2,1,0:T(8,128)S(1)} %get-tuple-element.8.last, bf16[128,192]{1,0:T(8,128)(2,1)S(1)} %copy-done), custom_call_target="tpu_custom_call" | custom-call | tf_op jit(solution)/shard_map/last_planes/pallas_call | solution.py:440
Async XLA Ops:
  0.0 57.0 %copy-start = (bf16[128,192]{1,0:T(8,128)(2,1)S(1)}, bf16[128,192]{1,0:T(8,128)(2,1)}, u32[]{:S(2)}) copy-start(bf16[128,192]{1,0:T(8,128)(2,1)} %constant.11.clone.inv_ref) | copy-start | bytes 147460
